TPU v7x, 32 devices: a whole 2x2x4 slice. The times are simulated.
32 devices in a mesh: grp: 2 (over y), band: 4 (over z), mem: 2 (over x), fld: 2 (over core).
Axes of the slice: x: 2, y: 2, z: 4, core: 2. Of those that a mesh axis runs over, the one named last changes fastest.
Arguments:
- surface_fields: bfloat16 [16, 8, 8, 65536], P(('grp', 'mem'), 'fld', None, 'band'), parts along dimension 0, may hold values from -8 to 8
- land_mask: int32 [65536], P('band'), may hold values from 0 to 1, as said below
- source_area: float32 [65536], P('band'), may hold values from 0.5 to 1.5
- target_area: float32 [16384], P('band'), may hold values from 0.75 to 1.25
- weight_tiles: bfloat16 [16, 128, 128], replicated, may hold values from -1 to 1
- tile_of: int32 [128, 24], P('band'), may hold values from 0 to 15
- block_of: int32 [128, 24], P('band'), may hold values from 0 to 191, as said below
- live_slots: int32 [128], P('band'), may hold values from 1 to 24, as said below
Outputs:
- regridded: float32 [16, 8, 8, 16384], P(('grp', 'mem'), 'fld', None, 'band'), parts along dimension 0
- conserved: float32 [16, 8, 8], P(('grp', 'mem'), 'fld'), parts along dimension 0
- ensemble: float32 [16, 8], P(('grp', 'fld')), parts along dimension 0
There are 2 independent parts, one for each index of `grp`. A program takes and returns all parts, laid end to end along the dimension named above; an argument that names none is the same for every part. Nothing has to cross between parts.
Inputs may be any that keep to these rules, and one draw needn't show every extreme that they name: `land_mask`: 1 marks ocean, 0 land. `block_of`: for the target block at place j (0 to 31) within its band, every entry lies in 4 * j to 4 * j + 4 + 2 * 32 - 1; values under 32 name the lower band's last blocks, values from 160 on the higher band's first blocks. `live_slots`: slots from this count on are unused.
All inputs are finite; a program needn't handle non-finite values.
Results may differ from a plain program's by a relative error of at most 0.0014.
Values may be sent and summed in bfloat16 or wider, within the bound.
A program may use at most 64 MiB of HBM per device.

v0:
```python
import jax
import jax.numpy as jnp
from jax import lax
from jax.sharding import PartitionSpec as P

MEMBERS = 8
HALO_BLK = 32


def extended_2(array, sides, width):
    for axis, dim in sides:
        size, length = (lax.axis_size(axis), array.shape[dim])
        up = [(i, (i + 1) % size) for i in range(size - 1)]
        down = [(j, i) for i, j in up]
        last = lax.slice_in_dim(array, length - width, length, axis=dim)
        leading = lax.slice_in_dim(array, 0, width, axis=dim)
        before = lax.ppermute(last, axis, up)
        after = lax.ppermute(leading, axis, down)
        array = jnp.concatenate([before, array, after], axis=dim)
    return array


def slot_terms(source, slot_names, weight_tiles, bounds):
    tile_ids, picked, usable, unused = slot_names
    columns = source.shape[0]
    tile_size = source.shape[2]
    tgt_count = picked.shape[0]

    def one_slot(position, running):
        chosen = jnp.take(source, picked[:, position], axis=1)
        weights = jnp.take(weight_tiles, tile_ids[:, position], axis=0)
        weights = jnp.where(
            usable[:, position][:, None, None], weights, jnp.zeros((), weight_tiles.dtype)
        )
        return running + jnp.einsum(
            "cnb,nbd->cnd", chosen, weights, preferred_element_type=jnp.float32
        )

    start = jnp.zeros((columns, tgt_count, tile_size), jnp.float32)
    return lax.fori_loop(bounds[0], bounds[1], one_slot, start)


def band_totals(own_total, target_part, area_part):
    return lax.psum((own_total, target_part, area_part), "band")


def on_device(
    surface_fields, land_mask, source_area, target_area, weight_tiles, tile_of, block_of, live_slots
):
    members, fields, snapshots, cell_count = surface_fields.shape
    columns = members * fields * snapshots
    tile_size = weight_tiles.shape[1]
    slot_count = tile_of.shape[1]
    tgt_count = tile_of.shape[0]
    own_blocks = cell_count // tile_size
    weighted = (
        source_area * land_mask.astype(jnp.float32) * surface_fields.astype(jnp.float32)
    ).astype(jnp.bfloat16)
    flat = weighted.reshape(columns, cell_count)
    own_total = jnp.sum(flat, axis=1, dtype=jnp.float32)
    area_part = jnp.sum(target_area)
    slot_place = lax.broadcasted_iota(jnp.int32, (tgt_count, slot_count), 1)
    slot_alive = slot_place < live_slots[:, None]
    extended = extended_2(flat, (("band", 1),), HALO_BLK * tile_size)
    source = extended.reshape(columns, own_blocks + 2 * HALO_BLK, tile_size)
    work_list = [(tile_of, block_of, slot_alive, live_slots)]
    results = [slot_terms(source, listed, weight_tiles, (0, slot_count)) for listed in work_list]
    raw_sums = results[0]
    raw_sums = raw_sums.reshape(columns, tgt_count * tile_size)
    totals = band_totals(own_total, jnp.sum(raw_sums, axis=1), area_part)
    source_total, target_total, area_total = totals
    correction = (source_total - target_total) / area_total
    regridded = raw_sums / target_area[None, :] + correction[:, None]
    conserved = (source_total / area_total).reshape(members, fields, snapshots)
    ensemble = lax.psum(jnp.sum(conserved, axis=0), "mem") / MEMBERS
    return (
        regridded.reshape(members, fields, snapshots, tgt_count * tile_size),
        conserved,
        ensemble,
    )


def solution(mesh):
    placed = (
        P(("grp", "mem"), "fld", None, "band"),
        P("band"),
        P("band"),
        P("band"),
        P(),
        P("band", None),
        P("band", None),
        P("band"),
    )
    return jax.shard_map(
        on_device,
        mesh=mesh,
        in_specs=placed,
        out_specs=(
            P(("grp", "mem"), "fld", None, "band"),
            P(("grp", "mem"), "fld", None),
            P(("grp", "fld"), None),
        ),
        check_vma=False,
    )
```

profile of v0, /device:TPU:0, one launch (start us, length us, event | category | flops | bytes accessed | tf_op | source)
XLA Modules:
  0.0 303.3 jit_solution(8360894486736070716)
XLA Ops:
  8.5 5.0 %collective-permute-start = (bf16[128,4096]{1,0:T(8,128)(2,1)}, bf16[128,4096]{1,0:T(8,128)(2,1)S(1)}, u32[]{:S(2)}, u32[]{:S(2)}) collective-permute-start(bf16[128,4096]{1,0:T(8,128)(2,1)} %get-tuple-element.191), channel_id=1, source_target_pairs={{0,4},{4,8},{8,12},{1,5},{5,9},{9,13},{2,6},{6,10},{10,14},{3,7},{... | collective-permute-start | bytes 3145736 | tf_op jit(solution)/shard_map/ppermute | solution.py:17
  15.5 20.6 %collective-permute-done = bf16[128,4096]{1,0:T(8,128)(2,1)S(1)} collective-permute-done((bf16[128,4096]{1,0:T(8,128)(2,1)}, bf16[128,4096]{1,0:T(8,128)(2,1)S(1)}, u32[]{:S(2)}, u32[]{:S(2)}) %collective-permute-start) | collective-permute-done | bytes 1048608 | tf_op jit(solution)/shard_map/ppermute | solution.py:17
  36.1 3.9 %collective-permute-done.1 = bf16[128,4096]{1,0:T(8,128)(2,1)S(1)} collective-permute-done((bf16[128,4096]{1,0:T(8,128)(2,1)S(1)}, bf16[128,4096]{1,0:T(8,128)(2,1)S(1)}, u32[]{:S(2)}, u32[]{:S(2)}) %collective-permute-start.1) | collective-permute-done | bytes 1048608 | tf_op jit(solution)/shard_map/ppermute | solution.py:18
  40.0 6.8 %pad_maximum_fusion = bf16[128,24576]{1,0:T(8,128)(2,1)} fusion(bf16[128,4096]{1,0:T(8,128)(2,1)S(1)} %collective-permute-done.1, bf16[128,16384]{1,0:T(8,128)(2,1)} %bitcast.28, bf16[128,4096]{1,0:T(8,128)(2,1)S(1)} %collective-permute-done), kind=kLoop, calls=%fused_computation.25 | loop fusion | flops 18874368 | bytes 12582912 | tf_op jit(solution)/shard_map/concatenate | solution.py:19
  46.8 8.6 %copy.21 = bf16[128,24576]{0,1:T(8,128)(2,1)} copy(bf16[128,24576]{1,0:T(8,128)(2,1)} %pad_maximum_fusion) | data formatting | bytes 12582912 | tf_op jit(solution)/shard_map/concatenate | solution.py:19
  55.4 8.7 %copy.22 = bf16[128,192,128]{2,0,1:T(8,128)(2,1)} copy(bf16[128,192,128]{0,2,1:T(8,128)(2,1)} %bitcast.29) | data formatting | bytes 12582912
  64.1 213.0 %while.14 = (s32[]{:T(128)}, f32[128,32,128]{0,2,1:T(8,128)}, pred[32,24]{0,1:T(8,128)(4,1)S(1)}, s32[32,24]{0,1:T(8,128)}, bf16[16,128,128]{2,1,0:T(8,128)(2,1)...) while((s32[]{:T(128)}, f32[128,32,128]{0,2,1:T(8,128)}, ...), condition=%wide.region_1.0_spmd.clone, body=%wide.region_0.0_spmd.clone.sunk | while | flops 136841600 | bytes 10495311 | solution.py:40
  76.5 3.9 %bitcast_add_fusion.2 = f32[128,32,128]{0,2,1:T(8,128)} fusion(f32[128,32,128]{0,2,1:T(8,128)} %get-tuple-element.256, bf16[32,128,128]{2,1,0:T(8,128)(2,1)S(1)} %gather_fusion, bf16[32,128,128]{2,1,0:T(8,128)(2,1)S(1)} %gather_fusion.1, pred[32]{0:T(512)(128)(4,1)S(1)} %get-tuple-element.244, pred[32]{0:T(512)(128)(4,1)S(1)} %get-tuple-element.245, ...), kind=kOutput, calls=%fused_computation.2.clone.1 | convolution fusion | flops 136839168 | bytes 6291553 | tf_op jit(solution)/shard_map/while/body/eval_jaxpr/cnb,nbd->cnd/dot_general | solution.py:35
  85.5 3.9 %bitcast_add_fusion.2 = f32[128,32,128]{0,2,1:T(8,128)} fusion(f32[128,32,128]{0,2,1:T(8,128)} %get-tuple-element.256, bf16[32,128,128]{2,1,0:T(8,128)(2,1)S(1)} %gather_fusion, bf16[32,128,128]{2,1,0:T(8,128)(2,1)S(1)} %gather_fusion.1, pred[32]{0:T(512)(128)(4,1)S(1)} %get-tuple-element.244, pred[32]{0:T(512)(128)(4,1)S(1)} %get-tuple-element.245, ...), kind=kOutput, calls=%fused_computation.2.clone.1 | convolution fusion | flops 136839168 | bytes 6291553 | tf_op jit(solution)/shard_map/while/body/eval_jaxpr/cnb,nbd->cnd/dot_general | solution.py:35
  94.4 3.9 %bitcast_add_fusion.2 = f32[128,32,128]{0,2,1:T(8,128)} fusion(f32[128,32,128]{0,2,1:T(8,128)} %get-tuple-element.256, bf16[32,128,128]{2,1,0:T(8,128)(2,1)S(1)} %gather_fusion, bf16[32,128,128]{2,1,0:T(8,128)(2,1)S(1)} %gather_fusion.1, pred[32]{0:T(512)(128)(4,1)S(1)} %get-tuple-element.244, pred[32]{0:T(512)(128)(4,1)S(1)} %get-tuple-element.245, ...), kind=kOutput, calls=%fused_computation.2.clone.1 | convolution fusion | flops 136839168 | bytes 6291553 | tf_op jit(solution)/shard_map/while/body/eval_jaxpr/cnb,nbd->cnd/dot_general | solution.py:35
  103.4 3.9 %bitcast_add_fusion.2 = f32[128,32,128]{0,2,1:T(8,128)} fusion(f32[128,32,128]{0,2,1:T(8,128)} %get-tuple-element.256, bf16[32,128,128]{2,1,0:T(8,128)(2,1)S(1)} %gather_fusion, bf16[32,128,128]{2,1,0:T(8,128)(2,1)S(1)} %gather_fusion.1, pred[32]{0:T(512)(128)(4,1)S(1)} %get-tuple-element.244, pred[32]{0:T(512)(128)(4,1)S(1)} %get-tuple-element.245, ...), kind=kOutput, calls=%fused_computation.2.clone.1 | convolution fusion | flops 136839168 | bytes 6291553 | tf_op jit(solution)/shard_map/while/body/eval_jaxpr/cnb,nbd->cnd/dot_general | solution.py:35
  112.3 3.9 %bitcast_add_fusion.2 = f32[128,32,128]{0,2,1:T(8,128)} fusion(f32[128,32,128]{0,2,1:T(8,128)} %get-tuple-element.256, bf16[32,128,128]{2,1,0:T(8,128)(2,1)S(1)} %gather_fusion, bf16[32,128,128]{2,1,0:T(8,128)(2,1)S(1)} %gather_fusion.1, pred[32]{0:T(512)(128)(4,1)S(1)} %get-tuple-element.244, pred[32]{0:T(512)(128)(4,1)S(1)} %get-tuple-element.245, ...), kind=kOutput, calls=%fused_computation.2.clone.1 | convolution fusion | flops 136839168 | bytes 6291553 | tf_op jit(solution)/shard_map/while/body/eval_jaxpr/cnb,nbd->cnd/dot_general | solution.py:35
  121.2 3.9 %bitcast_add_fusion.2 = f32[128,32,128]{0,2,1:T(8,128)} fusion(f32[128,32,128]{0,2,1:T(8,128)} %get-tuple-element.256, bf16[32,128,128]{2,1,0:T(8,128)(2,1)S(1)} %gather_fusion, bf16[32,128,128]{2,1,0:T(8,128)(2,1)S(1)} %gather_fusion.1, pred[32]{0:T(512)(128)(4,1)S(1)} %get-tuple-element.244, pred[32]{0:T(512)(128)(4,1)S(1)} %get-tuple-element.245, ...), kind=kOutput, calls=%fused_computation.2.clone.1 | convolution fusion | flops 136839168 | bytes 6291553 | tf_op jit(solution)/shard_map/while/body/eval_jaxpr/cnb,nbd->cnd/dot_general | solution.py:35
  130.2 3.9 %bitcast_add_fusion.2 = f32[128,32,128]{0,2,1:T(8,128)} fusion(f32[128,32,128]{0,2,1:T(8,128)} %get-tuple-element.256, bf16[32,128,128]{2,1,0:T(8,128)(2,1)S(1)} %gather_fusion, bf16[32,128,128]{2,1,0:T(8,128)(2,1)S(1)} %gather_fusion.1, pred[32]{0:T(512)(128)(4,1)S(1)} %get-tuple-element.244, pred[32]{0:T(512)(128)(4,1)S(1)} %get-tuple-element.245, ...), kind=kOutput, calls=%fused_computation.2.clone.1 | convolution fusion | flops 136839168 | bytes 6291553 | tf_op jit(solution)/shard_map/while/body/eval_jaxpr/cnb,nbd->cnd/dot_general | solution.py:35
  139.1 3.9 %bitcast_add_fusion.2 = f32[128,32,128]{0,2,1:T(8,128)} fusion(f32[128,32,128]{0,2,1:T(8,128)} %get-tuple-element.256, bf16[32,128,128]{2,1,0:T(8,128)(2,1)S(1)} %gather_fusion, bf16[32,128,128]{2,1,0:T(8,128)(2,1)S(1)} %gather_fusion.1, pred[32]{0:T(512)(128)(4,1)S(1)} %get-tuple-element.244, pred[32]{0:T(512)(128)(4,1)S(1)} %get-tuple-element.245, ...), kind=kOutput, calls=%fused_computation.2.clone.1 | convolution fusion | flops 136839168 | bytes 6291553 | tf_op jit(solution)/shard_map/while/body/eval_jaxpr/cnb,nbd->cnd/dot_general | solution.py:35
  148.1 3.9 %bitcast_add_fusion.2 = f32[128,32,128]{0,2,1:T(8,128)} fusion(f32[128,32,128]{0,2,1:T(8,128)} %get-tuple-element.256, bf16[32,128,128]{2,1,0:T(8,128)(2,1)S(1)} %gather_fusion, bf16[32,128,128]{2,1,0:T(8,128)(2,1)S(1)} %gather_fusion.1, pred[32]{0:T(512)(128)(4,1)S(1)} %get-tuple-element.244, pred[32]{0:T(512)(128)(4,1)S(1)} %get-tuple-element.245, ...), kind=kOutput, calls=%fused_computation.2.clone.1 | convolution fusion | flops 136839168 | bytes 6291553 | tf_op jit(solution)/shard_map/while/body/eval_jaxpr/cnb,nbd->cnd/dot_general | solution.py:35
  157.0 3.9 %bitcast_add_fusion.2 = f32[128,32,128]{0,2,1:T(8,128)} fusion(f32[128,32,128]{0,2,1:T(8,128)} %get-tuple-element.256, bf16[32,128,128]{2,1,0:T(8,128)(2,1)S(1)} %gather_fusion, bf16[32,128,128]{2,1,0:T(8,128)(2,1)S(1)} %gather_fusion.1, pred[32]{0:T(512)(128)(4,1)S(1)} %get-tuple-element.244, pred[32]{0:T(512)(128)(4,1)S(1)} %get-tuple-element.245, ...), kind=kOutput, calls=%fused_computation.2.clone.1 | convolution fusion | flops 136839168 | bytes 6291553 | tf_op jit(solution)/shard_map/while/body/eval_jaxpr/cnb,nbd->cnd/dot_general | solution.py:35
  166.0 3.9 %bitcast_add_fusion.2 = f32[128,32,128]{0,2,1:T(8,128)} fusion(f32[128,32,128]{0,2,1:T(8,128)} %get-tuple-element.256, bf16[32,128,128]{2,1,0:T(8,128)(2,1)S(1)} %gather_fusion, bf16[32,128,128]{2,1,0:T(8,128)(2,1)S(1)} %gather_fusion.1, pred[32]{0:T(512)(128)(4,1)S(1)} %get-tuple-element.244, pred[32]{0:T(512)(128)(4,1)S(1)} %get-tuple-element.245, ...), kind=kOutput, calls=%fused_computation.2.clone.1 | convolution fusion | flops 136839168 | bytes 6291553 | tf_op jit(solution)/shard_map/while/body/eval_jaxpr/cnb,nbd->cnd/dot_general | solution.py:35
  174.9 3.9 %bitcast_add_fusion.2 = f32[128,32,128]{0,2,1:T(8,128)} fusion(f32[128,32,128]{0,2,1:T(8,128)} %get-tuple-element.256, bf16[32,128,128]{2,1,0:T(8,128)(2,1)S(1)} %gather_fusion, bf16[32,128,128]{2,1,0:T(8,128)(2,1)S(1)} %gather_fusion.1, pred[32]{0:T(512)(128)(4,1)S(1)} %get-tuple-element.244, pred[32]{0:T(512)(128)(4,1)S(1)} %get-tuple-element.245, ...), kind=kOutput, calls=%fused_computation.2.clone.1 | convolution fusion | flops 136839168 | bytes 6291553 | tf_op jit(solution)/shard_map/while/body/eval_jaxpr/cnb,nbd->cnd/dot_general | solution.py:35
  183.8 3.9 %bitcast_add_fusion.2 = f32[128,32,128]{0,2,1:T(8,128)} fusion(f32[128,32,128]{0,2,1:T(8,128)} %get-tuple-element.256, bf16[32,128,128]{2,1,0:T(8,128)(2,1)S(1)} %gather_fusion, bf16[32,128,128]{2,1,0:T(8,128)(2,1)S(1)} %gather_fusion.1, pred[32]{0:T(512)(128)(4,1)S(1)} %get-tuple-element.244, pred[32]{0:T(512)(128)(4,1)S(1)} %get-tuple-element.245, ...), kind=kOutput, calls=%fused_computation.2.clone.1 | convolution fusion | flops 136839168 | bytes 6291553 | tf_op jit(solution)/shard_map/while/body/eval_jaxpr/cnb,nbd->cnd/dot_general | solution.py:35
  192.8 3.9 %bitcast_add_fusion.2 = f32[128,32,128]{0,2,1:T(8,128)} fusion(f32[128,32,128]{0,2,1:T(8,128)} %get-tuple-element.256, bf16[32,128,128]{2,1,0:T(8,128)(2,1)S(1)} %gather_fusion, bf16[32,128,128]{2,1,0:T(8,128)(2,1)S(1)} %gather_fusion.1, pred[32]{0:T(512)(128)(4,1)S(1)} %get-tuple-element.244, pred[32]{0:T(512)(128)(4,1)S(1)} %get-tuple-element.245, ...), kind=kOutput, calls=%fused_computation.2.clone.1 | convolution fusion | flops 136839168 | bytes 6291553 | tf_op jit(solution)/shard_map/while/body/eval_jaxpr/cnb,nbd->cnd/dot_general | solution.py:35
  201.7 3.9 %bitcast_add_fusion.2 = f32[128,32,128]{0,2,1:T(8,128)} fusion(f32[128,32,128]{0,2,1:T(8,128)} %get-tuple-element.256, bf16[32,128,128]{2,1,0:T(8,128)(2,1)S(1)} %gather_fusion, bf16[32,128,128]{2,1,0:T(8,128)(2,1)S(1)} %gather_fusion.1, pred[32]{0:T(512)(128)(4,1)S(1)} %get-tuple-element.244, pred[32]{0:T(512)(128)(4,1)S(1)} %get-tuple-element.245, ...), kind=kOutput, calls=%fused_computation.2.clone.1 | convolution fusion | flops 136839168 | bytes 6291553 | tf_op jit(solution)/shard_map/while/body/eval_jaxpr/cnb,nbd->cnd/dot_general | solution.py:35
  210.7 3.9 %bitcast_add_fusion.2 = f32[128,32,128]{0,2,1:T(8,128)} fusion(f32[128,32,128]{0,2,1:T(8,128)} %get-tuple-element.256, bf16[32,128,128]{2,1,0:T(8,128)(2,1)S(1)} %gather_fusion, bf16[32,128,128]{2,1,0:T(8,128)(2,1)S(1)} %gather_fusion.1, pred[32]{0:T(512)(128)(4,1)S(1)} %get-tuple-element.244, pred[32]{0:T(512)(128)(4,1)S(1)} %get-tuple-element.245, ...), kind=kOutput, calls=%fused_computation.2.clone.1 | convolution fusion | flops 136839168 | bytes 6291553 | tf_op jit(solution)/shard_map/while/body/eval_jaxpr/cnb,nbd->cnd/dot_general | solution.py:35
  219.6 3.9 %bitcast_add_fusion.2 = f32[128,32,128]{0,2,1:T(8,128)} fusion(f32[128,32,128]{0,2,1:T(8,128)} %get-tuple-element.256, bf16[32,128,128]{2,1,0:T(8,128)(2,1)S(1)} %gather_fusion, bf16[32,128,128]{2,1,0:T(8,128)(2,1)S(1)} %gather_fusion.1, pred[32]{0:T(512)(128)(4,1)S(1)} %get-tuple-element.244, pred[32]{0:T(512)(128)(4,1)S(1)} %get-tuple-element.245, ...), kind=kOutput, calls=%fused_computation.2.clone.1 | convolution fusion | flops 136839168 | bytes 6291553 | tf_op jit(solution)/shard_map/while/body/eval_jaxpr/cnb,nbd->cnd/dot_general | solution.py:35
  228.6 3.9 %bitcast_add_fusion.2 = f32[128,32,128]{0,2,1:T(8,128)} fusion(f32[128,32,128]{0,2,1:T(8,128)} %get-tuple-element.256, bf16[32,128,128]{2,1,0:T(8,128)(2,1)S(1)} %gather_fusion, bf16[32,128,128]{2,1,0:T(8,128)(2,1)S(1)} %gather_fusion.1, pred[32]{0:T(512)(128)(4,1)S(1)} %get-tuple-element.244, pred[32]{0:T(512)(128)(4,1)S(1)} %get-tuple-element.245, ...), kind=kOutput, calls=%fused_computation.2.clone.1 | convolution fusion | flops 136839168 | bytes 6291553 | tf_op jit(solution)/shard_map/while/body/eval_jaxpr/cnb,nbd->cnd/dot_general | solution.py:35
  237.5 3.9 %bitcast_add_fusion.2 = f32[128,32,128]{0,2,1:T(8,128)} fusion(f32[128,32,128]{0,2,1:T(8,128)} %get-tuple-element.256, bf16[32,128,128]{2,1,0:T(8,128)(2,1)S(1)} %gather_fusion, bf16[32,128,128]{2,1,0:T(8,128)(2,1)S(1)} %gather_fusion.1, pred[32]{0:T(512)(128)(4,1)S(1)} %get-tuple-element.244, pred[32]{0:T(512)(128)(4,1)S(1)} %get-tuple-element.245, ...), kind=kOutput, calls=%fused_computation.2.clone.1 | convolution fusion | flops 136839168 | bytes 6291553 | tf_op jit(solution)/shard_map/while/body/eval_jaxpr/cnb,nbd->cnd/dot_general | solution.py:35
  246.4 3.9 %bitcast_add_fusion.2 = f32[128,32,128]{0,2,1:T(8,128)} fusion(f32[128,32,128]{0,2,1:T(8,128)} %get-tuple-element.256, bf16[32,128,128]{2,1,0:T(8,128)(2,1)S(1)} %gather_fusion, bf16[32,128,128]{2,1,0:T(8,128)(2,1)S(1)} %gather_fusion.1, pred[32]{0:T(512)(128)(4,1)S(1)} %get-tuple-element.244, pred[32]{0:T(512)(128)(4,1)S(1)} %get-tuple-element.245, ...), kind=kOutput, calls=%fused_computation.2.clone.1 | convolution fusion | flops 136839168 | bytes 6291553 | tf_op jit(solution)/shard_map/while/body/eval_jaxpr/cnb,nbd->cnd/dot_general | solution.py:35
  255.4 3.9 %bitcast_add_fusion.2 = f32[128,32,128]{0,2,1:T(8,128)} fusion(f32[128,32,128]{0,2,1:T(8,128)} %get-tuple-element.256, bf16[32,128,128]{2,1,0:T(8,128)(2,1)S(1)} %gather_fusion, bf16[32,128,128]{2,1,0:T(8,128)(2,1)S(1)} %gather_fusion.1, pred[32]{0:T(512)(128)(4,1)S(1)} %get-tuple-element.244, pred[32]{0:T(512)(128)(4,1)S(1)} %get-tuple-element.245, ...), kind=kOutput, calls=%fused_computation.2.clone.1 | convolution fusion | flops 136839168 | bytes 6291553 | tf_op jit(solution)/shard_map/while/body/eval_jaxpr/cnb,nbd->cnd/dot_general | solution.py:35
  264.3 3.9 %bitcast_add_fusion.2 = f32[128,32,128]{0,2,1:T(8,128)} fusion(f32[128,32,128]{0,2,1:T(8,128)} %get-tuple-element.256, bf16[32,128,128]{2,1,0:T(8,128)(2,1)S(1)} %gather_fusion, bf16[32,128,128]{2,1,0:T(8,128)(2,1)S(1)} %gather_fusion.1, pred[32]{0:T(512)(128)(4,1)S(1)} %get-tuple-element.244, pred[32]{0:T(512)(128)(4,1)S(1)} %get-tuple-element.245, ...), kind=kOutput, calls=%fused_computation.2.clone.1 | convolution fusion | flops 136839168 | bytes 6291553 | tf_op jit(solution)/shard_map/while/body/eval_jaxpr/cnb,nbd->cnd/dot_general | solution.py:35
  273.3 3.9 %bitcast_add_fusion.2 = f32[128,32,128]{0,2,1:T(8,128)} fusion(f32[128,32,128]{0,2,1:T(8,128)} %get-tuple-element.256, bf16[32,128,128]{2,1,0:T(8,128)(2,1)S(1)} %gather_fusion, bf16[32,128,128]{2,1,0:T(8,128)(2,1)S(1)} %gather_fusion.1, pred[32]{0:T(512)(128)(4,1)S(1)} %get-tuple-element.244, pred[32]{0:T(512)(128)(4,1)S(1)} %get-tuple-element.245, ...), kind=kOutput, calls=%fused_computation.2.clone.1 | convolution fusion | flops 136839168 | bytes 6291553 | tf_op jit(solution)/shard_map/while/body/eval_jaxpr/cnb,nbd->cnd/dot_general | solution.py:35
  281.7 10.5 %all-reduce = (f32[128]{0:T(128)S(1)}, f32[128]{0:T(128)S(1)}, f32[]{:T(128)}) all-reduce(f32[128]{0:T(128)S(1)} %reduce_sum.39, f32[128]{0:T(128)S(1)} %reduce_sum.40, f32[]{:T(128)} %reduce_sum.41), channel_id=1, replica_groups=mesh['grp'=2,'band'=4,'mem'=2,'fld'=2] {'band'}, use_global_device_ids=true, to_apply=%region_3.0 | all-reduce | flops 257 | bytes 2056 | tf_op jit(solution)/shard_map/psum | solution.py:44
  294.6 4.9 %psum.31 = f32[4,8]{1,0:T(4,128)S(1)} all-reduce(f32[4,8]{1,0:T(4,128)S(1)} %reduce_sum.42), channel_id=1, replica_groups=mesh['grp'=2,'band'=4,'mem'=2,'fld'=2] {'mem'}, use_global_device_ids=true, to_apply=%region_9.10 | all-reduce | flops 32 | bytes 256 | tf_op jit(solution)/shard_map/psum | solution.py:75
  (172 shorter events, 143.3 us)
Async XLA Ops:
  5.3 2.0 copy-start.1
  5.3 9.6 %copy-start.2 = (f32[4096]{0:T(1024)S(1)}, f32[4096]{0:T(1024)}, u32[]{:S(2)}) copy-start(f32[4096]{0:T(1024)} %param.13) | copy-start | bytes 49156
  5.3 10.2 %copy-start.4 = (s32[32]{0:T(128)S(1)}, s32[32]{0:T(128)}, u32[]{:S(2)}) copy-start(s32[32]{0:T(128)} %param.17) | copy-start | bytes 388
  8.5 27.7 %collective-permute-start = (bf16[128,4096]{1,0:T(8,128)(2,1)}, bf16[128,4096]{1,0:T(8,128)(2,1)S(1)}, u32[]{:S(2)}, u32[]{:S(2)}) collective-permute-start(bf16[128,4096]{1,0:T(8,128)(2,1)} %get-tuple-element.191), channel_id=1, source_target_pairs={{0,4},{4,8},{8,12},{1,5},{5,9},{9,13},{2,6},{6,10},{10,14},{3,7},{... | collective-permute-start | bytes 3145736 | tf_op jit(solution)/shard_map/ppermute | solution.py:17
  13.5 26.5 %collective-permute-start.1 = (bf16[128,4096]{1,0:T(8,128)(2,1)S(1)}, bf16[128,4096]{1,0:T(8,128)(2,1)S(1)}, u32[]{:S(2)}, u32[]{:S(2)}) collective-permute-start(bf16[128,4096]{1,0:T(8,128)(2,1)S(1)} %get-tuple-element.192), channel_id=1, source_target_pairs={{4,0},{8,4},{12,8},{5,1},{9,5},{13,9},{6,2},{10,6},{14,10},{7,3},{... | collective-permute-start | bytes 3145736 | tf_op jit(solution)/shard_map/ppermute | solution.py:18
  55.4 8.7 %copy-start = (bf16[16,128,128]{2,1,0:T(8,128)(2,1)S(1)}, bf16[16,128,128]{2,1,0:T(8,128)(2,1)}, u32[]{:S(2)}) copy-start(bf16[16,128,128]{2,1,0:T(8,128)(2,1)} %param.14) | copy-start | bytes 1572868
  294.6 8.7 %copy-start.3 = (f32[4,4,8]{2,1,0:T(4,128)}, f32[4,4,8]{2,1,0:T(4,128)S(1)}, u32[]{:S(2)}) copy-start(f32[4,4,8]{2,1,0:T(4,128)S(1)} %reshape.51) | copy-start | bytes 1540
where the time goes:
time: 306 us; the launch traced here: 303 us
  local copies, waits for them, and re-layouts  128 us (42%)
  matrix products  91.6 us (30%)
  other arithmetic  35.9 us (12%)
  waiting for transfers between devices  24.5 us (8%)
  blocking collectives  15.5 us (5%)
  starting transfers between devices  6.3 us (2%)
    dot_general x24, matrix products, one_slot(): jnp.einsum('cnb,nbd->cnd', chosen, weights, preferred_element_type=jnp.fl...  91.6 us
    gather x24, local copies, waits for them, and re-layouts, one_slot(): chosen = jnp.take(source, picked[:, position], axis=1)  84.8 us
    ppermute x1, waiting for transfers between devices, extended_2(): before = lax.ppermute(last, axis, up)  20.6 us
    gather x24, local copies, waits for them, and re-layouts, one_slot(): weights = jnp.take(weight_tiles, tile_ids[:, position], axis=0)  18 us
    reduce_and x24, other arithmetic, one_slot(): chosen = jnp.take(source, picked[:, position], axis=1)  17.1 us
    unnamed x11, local copies, waits for them, and re-layouts  10.8 us
    psum x1, blocking collectives, band_totals(): return lax.psum((own_total, target_part, area_part), 'band')  10.5 us
    concatenate x1, local copies, waits for them, and re-layouts, extended_2(): array = jnp.concatenate([before, array, after], axis=dim)  8.62 us
  transfers between devices with their start and end apart: 2, of which 2 were waited for; matrix products, arithmetic and copies ran while one was open for 0% of the time, Pallas kernels for 0%

commit v1 on v0

v1 whole, which is shorter than its diff:
```python
import functools

import jax
import jax.numpy as jnp
from jax import lax
from jax.experimental import pallas as pl
from jax.experimental.pallas import tpu as pltpu
from jax.sharding import PartitionSpec as P

HALO_BLK = 32
GROUP = 8
SEND_TYPE = jnp.float32
MESH = pl.DeviceIdType.MESH
VMEM = pl.BlockSpec(memory_space=pltpu.VMEM)
SMEM = pl.BlockSpec(memory_space=pltpu.SMEM)


def row_of(sums):
    return jnp.sum(sums.T, axis=0, keepdims=True)


def weigh_kernel(tile, fields_ref, mask_ref, area_ref, out_ref, total_ref):
    scale = area_ref[...] * mask_ref[...].astype(jnp.float32)
    columns = total_ref.shape[0]

    @pl.when(pl.program_id(0) == 0)
    def _():
        total_ref[...] = jnp.zeros_like(total_ref)

    running = total_ref[...]
    for n in range(out_ref.shape[0]):
        part = fields_ref[:, :, n * tile:(n + 1) * tile].astype(jnp.float32)
        part = part.reshape(columns, tile) * scale[:, n * tile:(n + 1) * tile]
        part = part.astype(jnp.bfloat16)
        out_ref[n] = part
        running = running + part.astype(jnp.float32)
    total_ref[...] = running


def weigh(fields, mask, area, tile, steps):
    rows, snaps, cells = fields.shape
    columns, blocks = rows * snaps, cells // tile
    chunk = cells // steps
    return pl.pallas_call(
        functools.partial(weigh_kernel, tile),
        grid=(steps,),
        in_specs=[
            pl.BlockSpec((rows, snaps, chunk), lambda i: (0, 0, i)),
            pl.BlockSpec((1, chunk), lambda i: (0, i)),
            pl.BlockSpec((1, chunk), lambda i: (0, i)),
        ],
        out_specs=(
            pl.BlockSpec((blocks // steps, columns, tile), lambda i: (i, 0, 0)),
            pl.BlockSpec((columns, tile), lambda i: (0, 0)),
        ),
        out_shape=(
            jax.ShapeDtypeStruct((blocks, columns, tile), jnp.bfloat16),
            jax.ShapeDtypeStruct((columns, tile), jnp.float32),
        ),
        cost_estimate=pl.CostEstimate(
            flops=4 * columns * cells, bytes_accessed=4 * columns * cells, transcendentals=0
        ),
    )(fields, mask, area)


def list_pairs(first, count, slots, table, shift, low, high, zero_tile, lists, start):
    tiles, blocks, live = table
    list_b, list_w, list_t = lists

    def one_target(n, place):
        used = live(n)
        for i in range(slots // 2 + 1):
            list_t[place // 2 + i] = first + n
        for k in range(slots):
            block = blocks(n, k) - shift
            keep = (k < used) & (block >= low) & (block < high)
            list_b[place] = block
            list_w[place] = tiles(n, k)
            place = place + keep.astype(jnp.int32)
        list_b[place] = low
        list_w[place] = zero_tile
        return place + lax.rem(place, 2)

    return lax.fori_loop(0, count, one_target, start)


def run_pairs(source, tiles, lists, entries, zero_tile, low, acc):
    list_b, list_w, list_t = lists
    for i in range(2 * GROUP):
        list_b[entries + i] = low
        list_w[entries + i] = zero_tile
    for i in range(GROUP):
        list_t[entries // 2 + i] = 0

    def one_group(g, carry):
        for u in range(GROUP):
            p = g * GROUP + u
            left = jnp.concatenate(
                [source[list_b[2 * p]], source[list_b[2 * p + 1]]], axis=1
            )
            right = jnp.concatenate(
                [tiles[list_w[2 * p]], tiles[list_w[2 * p + 1]]], axis=0
            )
            t = list_t[p]
            acc[t] = acc[t] + jnp.dot(left, right, preferred_element_type=jnp.float32)
        return carry

    lax.fori_loop(0, (entries // 2 + GROUP - 1) // GROUP, one_group, 0)


def fill_tiles(tiles_ref, held):
    count = tiles_ref.shape[0]
    held[0:count] = tiles_ref[...]
    held[count] = jnp.zeros(held.shape[1:], held.dtype)


def edge_kernel(
    edge, slots, own, upper_ref, lower_ref, source, tiles_ref, up_ref, down_ref, sum_ref,
    held, acc, list_b, list_w, list_t,
):
    fill_tiles(tiles_ref, held)
    zero_tile = tiles_ref.shape[0]
    acc[...] = jnp.zeros_like(acc)
    lists = (list_b, list_w, list_t)

    def table(ref):
        return (
            lambda n, k: ref[n, k],
            lambda n, k: ref[n, slots + k],
            lambda n: ref[n, 2 * slots],
        )

    place = list_pairs(
        0, edge, slots, table(upper_ref), HALO_BLK - own, own - HALO_BLK, own, zero_tile, lists, 0
    )
    place = list_pairs(
        edge, edge, slots, table(lower_ref), own + HALO_BLK, 0, HALO_BLK, zero_tile, lists, place
    )
    run_pairs(source, held, lists, place, zero_tile, 0, acc)
    up_ref[...] = acc[0:edge].astype(up_ref.dtype)
    down_ref[...] = acc[edge:2 * edge].astype(down_ref.dtype)
    sum_ref[...] = jnp.sum(acc[...], axis=0)


def list_scratch(targets, slots):
    size = targets * (slots + 2) + 4 * GROUP + slots
    return [
        pltpu.SMEM((size,), jnp.int32),
        pltpu.SMEM((size,), jnp.int32),
        pltpu.SMEM((size,), jnp.int32),
    ]


def edges(upper, lower, source, tiles, edge, slots):
    own, columns, tile = source.shape
    part = jax.ShapeDtypeStruct((edge, columns, tile), SEND_TYPE)
    return pl.pallas_call(
        functools.partial(edge_kernel, edge, slots, own),
        in_specs=[SMEM, SMEM, VMEM, VMEM],
        out_specs=(VMEM, VMEM, VMEM),
        out_shape=(part, part, jax.ShapeDtypeStruct((columns, tile), jnp.float32)),
        scratch_shapes=[
            pltpu.VMEM((tiles.shape[0] + 1, tile, tile), tiles.dtype),
            pltpu.VMEM((2 * edge, columns, tile), jnp.float32),
        ] + list_scratch(2 * edge, slots),
        cost_estimate=pl.CostEstimate(
            flops=2 * 4 * edge * columns * tile * tile, bytes_accessed=4 << 20, transcendentals=0
        ),
    )(upper, lower, source, tiles)


def own_kernel(
    tile_of, block_of, live_ref, source, tiles_ref, src_ref, edge_ref, area_ref, raw_ref, row_ref,
    held, list_b, list_w, list_t,
):
    targets, slots = tile_of.shape
    own = source.shape[0]
    zero_tile = tiles_ref.shape[0]
    fill_tiles(tiles_ref, held)
    raw_ref[...] = jnp.zeros_like(raw_ref)
    lists = (list_b, list_w, list_t)
    table = (
        lambda n, k: tile_of[n, k],
        lambda n, k: block_of[n, k],
        lambda n: live_ref[n],
    )
    place = list_pairs(0, targets, slots, table, HALO_BLK, 0, own, zero_tile, lists, 0)
    run_pairs(source, held, lists, place, zero_tile, 0, raw_ref)
    columns = src_ref.shape[0]
    row_ref[0:1, :] = row_of(src_ref[...])
    row_ref[1:2, :] = row_of(jnp.sum(raw_ref[...], axis=0) + edge_ref[...])
    row_ref[2:3, :] = jnp.broadcast_to(jnp.sum(area_ref[...], axis=1, keepdims=True), (1, columns))
    row_ref[3:8, :] = jnp.zeros((5, columns), jnp.float32)


def own_targets(tile_of, block_of, live, source, tiles, src_sum, edge_sum, area):
    own, columns, tile = source.shape
    targets, slots = tile_of.shape
    return pl.pallas_call(
        own_kernel,
        in_specs=[SMEM, SMEM, SMEM, VMEM, VMEM, VMEM, VMEM, VMEM],
        out_specs=(VMEM, VMEM),
        out_shape=(
            jax.ShapeDtypeStruct((targets, columns, tile), jnp.float32),
            jax.ShapeDtypeStruct((8, columns), jnp.float32),
        ),
        scratch_shapes=[pltpu.VMEM((tiles.shape[0] + 1, tile, tile), tiles.dtype)]
        + list_scratch(targets, slots),
        cost_estimate=pl.CostEstimate(
            flops=2 * targets * slots * columns * tile * tile,
            bytes_accessed=6 << 20,
            transcendentals=0,
        ),
    )(tile_of, block_of, live, source, tiles, src_sum, edge_sum, area)


def totals_kernel(bands, mems, row_ref, out_ref, fix_ref, landed, send_sem, recv_sem):
    band, mem = lax.axis_index("band"), lax.axis_index("mem")
    count = bands * mems
    me = mem * bands + band

    def place(step):
        other = lax.rem(me + step, count)
        return other, {"mem": other // bands, "band": lax.rem(other, bands)}

    barrier = pltpu.get_barrier_semaphore()

    def greet(step, carry):
        pl.semaphore_signal(barrier, inc=1, device_id=place(step)[1], device_id_type=MESH)
        return carry

    lax.fori_loop(1, count, greet, 0)
    pl.semaphore_wait(barrier, count - 1)

    def copy(step):
        return pltpu.make_async_remote_copy(
            src_ref=row_ref,
            dst_ref=landed.at[step],
            send_sem=send_sem.at[step],
            recv_sem=recv_sem.at[step],
            device_id=place(step)[1],
            device_id_type=MESH,
        )

    def begin(step, carry):
        copy(step).start()
        return carry

    def finish(step, carry):
        copy(step).wait()
        return carry

    lax.fori_loop(1, count, begin, 0)
    landed[0] = row_ref[...]
    lax.fori_loop(1, count, finish, 0)
    for m in range(mems):
        total = jnp.zeros(row_ref.shape, jnp.float32)
        for b in range(bands):
            sender = m * bands + b
            total = total + landed[lax.rem(me - sender + count, count)]
        out_ref[m] = total
    mine = out_ref[mem]
    fix = (mine[0:1, :] - mine[1:2, :]) / mine[2:3, :]
    fix_ref[...] = jnp.broadcast_to(fix, (fix_ref.shape[1], fix.shape[1])).T


def exchange_totals(rows, tile):
    bands, mems = lax.axis_size("band"), lax.axis_size("mem")
    columns = rows.shape[1]
    return pl.pallas_call(
        functools.partial(totals_kernel, bands, mems),
        in_specs=[VMEM],
        out_specs=(VMEM, VMEM),
        out_shape=(
            jax.ShapeDtypeStruct((mems, 8, columns), jnp.float32),
            jax.ShapeDtypeStruct((columns, tile), jnp.float32),
        ),
        scratch_shapes=[
            pltpu.VMEM((bands * mems, 8, columns), jnp.float32),
            pltpu.SemaphoreType.DMA((bands * mems,)),
            pltpu.SemaphoreType.DMA((bands * mems,)),
        ],
        compiler_params=pltpu.CompilerParams(collective_id=0, has_side_effects=True),
    )(rows)


def finish_kernel(raw_ref, low_ref, high_ref, area_ref, fix_ref, out_ref):
    step, last = pl.program_id(0), pl.num_programs(0) - 1
    count, columns, tile = raw_ref.shape
    use_low = step == 0
    use_high = step == last
    for n in range(count):
        value = raw_ref[n]
        value = value + jnp.where(use_low, low_ref[n].astype(jnp.float32), 0.0)
        value = value + jnp.where(use_high, high_ref[n].astype(jnp.float32), 0.0)
        value = value / area_ref[:, n * tile:(n + 1) * tile] + fix_ref[...]
        out_ref[:, :, n * tile:(n + 1) * tile] = value.reshape(out_ref.shape[0], out_ref.shape[1], tile)


def finish(raw, low, high, area, fix, rows, snaps):
    targets, columns, tile = raw.shape
    edge = low.shape[0]
    return pl.pallas_call(
        finish_kernel,
        grid=(targets // edge,),
        in_specs=[
            pl.BlockSpec((edge, columns, tile), lambda i: (i, 0, 0)),
            pl.BlockSpec((edge, columns, tile), lambda i: (0, 0, 0)),
            pl.BlockSpec((edge, columns, tile), lambda i: (0, 0, 0)),
            pl.BlockSpec((1, edge * tile), lambda i: (0, i)),
            pl.BlockSpec((columns, tile), lambda i: (0, 0)),
        ],
        out_specs=pl.BlockSpec((rows, snaps, edge * tile), lambda i: (0, 0, i)),
        out_shape=jax.ShapeDtypeStruct((rows, snaps, targets * tile), jnp.float32),
    )(raw, low, high, area, fix)


def on_device(
    surface_fields, land_mask, source_area, target_area, weight_tiles, tile_of, block_of, live_slots
):
    members, fields, snaps, cells = surface_fields.shape
    tile = weight_tiles.shape[1]
    targets, slots = tile_of.shape
    own = cells // tile
    edge = HALO_BLK // (own // targets)
    bands = lax.axis_size("band")
    up = [(i, i + 1) for i in range(bands - 1)]
    down = [(j, i) for i, j in up]

    table = jnp.concatenate([tile_of, block_of, live_slots[:, None]], axis=1)
    upper = lax.ppermute(table[:edge], "band", down)
    lower = lax.ppermute(table[targets - edge:], "band", up)

    area = target_area.reshape(1, targets * tile)
    source, src_sum = weigh(
        surface_fields.reshape(members * fields, snaps, cells),
        land_mask.reshape(1, cells),
        source_area.reshape(1, cells),
        tile,
        8,
    )
    to_upper, to_lower, edge_sum = edges(upper, lower, source, weight_tiles, edge, slots)
    low = lax.ppermute(to_upper, "band", up)
    high = lax.ppermute(to_lower, "band", down)
    raw, rows = own_targets(
        tile_of, block_of, live_slots, source, weight_tiles, src_sum, edge_sum, area
    )
    totals, fix = exchange_totals(rows, tile)
    regridded = finish(raw, low, high, area, fix, members * fields, snaps)
    means = totals[:, 0] / totals[:, 2]
    conserved = lax.dynamic_index_in_dim(means, lax.axis_index("mem"), 0, keepdims=False)
    mems = means.shape[0]
    ensemble = jnp.sum(means.reshape(mems * members, fields, snaps), axis=0) / (mems * members)
    return (
        regridded.reshape(members, fields, snaps, targets * tile),
        conserved.reshape(members, fields, snaps),
        ensemble,
    )


def solution(mesh):
    placed = (
        P(("grp", "mem"), "fld", None, "band"),
        P("band"),
        P("band"),
        P("band"),
        P(),
        P("band", None),
        P("band", None),
        P("band"),
    )
    return jax.shard_map(
        on_device,
        mesh=mesh,
        in_specs=placed,
        out_specs=(
            P(("grp", "mem"), "fld", None, "band"),
            P(("grp", "mem"), "fld", None),
            P(("grp", "fld"), None),
        ),
        check_vma=False,
    )
```

time: 306 us -> 61.4 us (0.20)
  local copies, waits for them, and re-layouts: 128 us -> 5.19 us
  matrix products: 91.6 us -> 0 us
  Pallas kernels: 0 us -> 40.8 us
  other arithmetic: 35.9 us -> 2.12 us
  waiting for transfers between devices: 24.5 us -> 0.01 us
  blocking collectives: 15.5 us -> 0 us
  starting transfers between devices: 6.3 us -> 12.7 us
    gather x48 -> x0, local copies, waits for them, and re-layouts: 103 us -> none  [the longest x24 84.8 us: one_slot(): chosen = jnp.take(source, picked[:, position], axis=1)]
    dot_general x24 -> x0, matrix products: 91.6 us -> none  [one_slot(): jnp.einsum('cnb,nbd->cnd', chosen, weights, preferred_element_type=jnp.fl...]
    pallas_call x0 -> x5, Pallas kernels: none -> 40.8 us  [the longest x1 12.5 us: exchange_totals(): pl.pallas_call(functools.partial(totals_kernel, bands, mems), in_specs=[V...]
    ppermute x2 -> x4, waiting for transfers between devices: 24.5 us -> 0.01 us  [the longest x1 0.01 us: on_device(): lower = lax.ppermute(table[targets - edge:], 'band', up)]
    reduce_and x24 -> x0, other arithmetic: 17.1 us -> none  [one_slot(): chosen = jnp.take(source, picked[:, position], axis=1)]
    psum x2 -> x0, blocking collectives: 15.5 us -> none  [the longest x1 10.5 us: band_totals(): return lax.psum((own_total, target_part, area_part), 'band')]
    concatenate x1 -> x0, local copies, waits for them, and re-layouts: 8.62 us -> none  [extended_2(): array = jnp.concatenate([before, array, after], axis=dim)]
    unnamed x11 -> x14, local copies, waits for them, and re-layouts: 10.8 us -> 3.11 us
  transfers between devices with their start and end apart: 2 -> 4, of which waited for: 2 -> 0; matrix products, arithmetic and copies ran while one was open for 0% -> 5% of each run, Pallas kernels for 0% -> 50%
where the time goes in v1:
time: 61.4 us; the launch traced here: 61.6 us
  Pallas kernels  40.8 us (66%)
  starting transfers between devices  12.7 us (21%)
  local copies, waits for them, and re-layouts  5.19 us (8%)
  other arithmetic  2.12 us (3%)
  between operations  0.74 us (1%)
    pallas_call x1, Pallas kernels, exchange_totals(): pl.pallas_call(functools.partial(totals_kernel, bands, mems), in_specs=[V...  12.5 us
    pallas_call x1, Pallas kernels, own_targets(): pl.pallas_call(own_kernel, in_specs=[SMEM, SMEM, SMEM, VMEM, VMEM, VMEM,...  11.2 us
    pallas_call x1, Pallas kernels, weigh(): pl.pallas_call(functools.partial(weigh_kernel, tile), grid=(steps,), in_s...  6.92 us
    pallas_call x1, Pallas kernels, edges(): pl.pallas_call(functools.partial(edge_kernel, edge, slots, own), in_specs...  5.88 us
    ppermute x1, starting transfers between devices, on_device(): lower = lax.ppermute(table[targets - edge:], 'band', up)  5.58 us
    ppermute x1, starting transfers between devices, on_device(): low = lax.ppermute(to_upper, 'band', up)  4.54 us
    pallas_call x1, Pallas kernels, finish(): pl.pallas_call(finish_kernel, grid=(targets // edge,), in_specs=[pl.Block...  4.24 us
    unnamed x14, local copies, waits for them, and re-layouts  3.11 us
  transfers between devices with their start and end apart: 4, of which 0 were waited for; matrix products, arithmetic and copies ran while one was open for 5% of the time, Pallas kernels for 50%

profile of v1, /device:TPU:0, one launch (start us, length us, event | category | flops | bytes accessed | tf_op | source)
XLA Modules:
  0.0 61.6 jit_solution(286501120563070970)
XLA Ops:
  0.6 0.8 %copy.14.tile_of = s32[32,24]{1,0:T(8,128)S(1)} copy(s32[32,24]{0,1:T(8,128)} %param.13) | data formatting | bytes 6144 | tf_op args[5]
  1.4 0.0 copy-start.2
  1.4 0.8 %copy.15.block_of = s32[32,24]{1,0:T(8,128)S(1)} copy(s32[32,24]{0,1:T(8,128)} %param.14) | data formatting | bytes 6144 | tf_op args[6]
  2.2 0.7 %copy.13 = s32[32,1]{1,0:T(8,128)S(1)} copy(s32[32,1]{0,1:T(1,128)} %bitcast.12) | data formatting | bytes 256 | tf_op jit(solution)/shard_map/broadcast_in_dim | solution.py:330
  2.9 0.1 pad_add_fusion
  3.0 1.3 %collective-permute-start = (s32[8,49]{1,0:T(8,128)S(1)}, s32[8,49]{1,0:T(8,128)S(1)}, u32[]{:S(2)}, u32[]{:S(2)}) collective-permute-start(s32[8,49]{1,0:T(8,128)S(1)} %get-tuple-element.24), channel_id=1, source_target_pairs={{4,0},{8,4},{12,8},{5,1},{9,5},{13,9},{6,2},{10,6},{14,10},{7,3},{... | collective-permute-start | bytes 4712 | tf_op jit(solution)/shard_map/ppermute | solution.py:331
  4.3 5.6 %collective-permute-start.1 = (s32[8,49]{1,0:T(8,128)S(1)}, s32[8,49]{1,0:T(8,128)S(1)}, u32[]{:S(2)}, u32[]{:S(2)}) collective-permute-start(s32[8,49]{1,0:T(8,128)S(1)} %get-tuple-element.23), channel_id=1, source_target_pairs={{0,4},{4,8},{8,12},{1,5},{5,9},{9,13},{2,6},{6,10},{10,14},{3,7},{... | collective-permute-start | bytes 4712 | tf_op jit(solution)/shard_map/ppermute | solution.py:332
  9.9 6.9 %shard_map.103 = (bf16[128,128,128]{2,1,0:T(8,128)(2,1)}, f32[128,128]{1,0:T(8,128)}) custom-call(bf16[16,8,16384]{2,1,0:T(8,128)(2,1)} %bitcast.6, s32[1,16384]{1,0:T(1,128)} %bitcast.8, f32[1,16384]{1,0:T(1,128)} %bitcast.9), custom_call_target="tpu_custom_call" | custom-call | flops 8388608 | bytes 8388608 | tf_op jit(solution)/shard_map/pallas_call | solution.py:44
  16.8 0.0 collective-permute-done.upper_ref
  16.8 0.0 copy-start.4
  16.9 0.0 collective-permute-done.1.lower_ref
  16.9 0.0 copy-start.5
  16.9 0.6 copy-done.4
  17.4 0.0 copy-done.5
  17.5 5.9 %shard_map.104 = (f32[8,128,128]{2,1,0:T(8,128)}, f32[8,128,128]{2,1,0:T(8,128)}, f32[128,128]{1,0:T(8,128)}) custom-call(s32[8,49]{1,0:T(8,128)} %copy-done.4, s32[8,49]{1,0:T(8,128)} %copy-done.5, bf16[128,128,128]{2,1,0:T(8,128)(2,1)} %get-tuple-element.12.source, bf16[16,128,128]{2,1,0:T(8,128)(2,1)} %tiles_ref.3), custom_call_target="tpu_custom_call" | custom-call | flops 134217728 | bytes 4194304 | tf_op jit(solution)/shard_map/pallas_call | solution.py:157
  23.3 0.0 copy-done.2
  23.3 0.0 copy-done.3
  23.4 4.5 %collective-permute-start.2 = (f32[8,128,128]{2,1,0:T(8,128)}, f32[8,128,128]{2,1,0:T(8,128)S(1)}, u32[]{:S(2)}, u32[]{:S(2)}) collective-permute-start(f32[8,128,128]{2,1,0:T(8,128)} %get-tuple-element.16), channel_id=1, source_target_pairs={{0,4},{4,8},{8,12},{1,5},{5,9},{9,13},{2,6},{6,10},{10,14},{3,7},{... | collective-permute-start | bytes 1572872 | tf_op jit(solution)/shard_map/ppermute | solution.py:343
  27.9 1.3 %collective-permute-start.3 = (f32[8,128,128]{2,1,0:T(8,128)}, f32[8,128,128]{2,1,0:T(8,128)S(1)}, u32[]{:S(2)}, u32[]{:S(2)}) collective-permute-start(f32[8,128,128]{2,1,0:T(8,128)} %get-tuple-element.17), channel_id=1, source_target_pairs={{4,0},{8,4},{12,8},{5,1},{9,5},{13,9},{6,2},{10,6},{14,10},{7,3},{... | collective-permute-start | bytes 1572872 | tf_op jit(solution)/shard_map/ppermute | solution.py:344
  29.2 11.2 %shard_map.105 = (f32[32,128,128]{2,1,0:T(8,128)}, f32[8,128]{1,0:T(8,128)}) custom-call(s32[32,24]{1,0:T(8,128)} %copy-done.2, s32[32,24]{1,0:T(8,128)} %copy-done.3, s32[32]{0:T(128)} %live_ref.1, bf16[128,128,128]{2,1,0:T(8,128)(2,1)} %get-tuple-element.12.source, bf16[16,128,128]{2,1,0:T(8,128)(2,1)} %tiles_ref.3, f32[128,128]{1,0:T(8,128)} %get-tuple-element.13.src_ref, ...), custom_call_target="tpu_custom_call" | custom-call | flops 3221225472 | bytes 6291456 | tf_op jit(solution)/shard_map/pallas_call | solution.py:199
  40.4 12.5 %shard_map.106 = (f32[2,8,128]{2,1,0:T(8,128)}, f32[128,128]{1,0:T(8,128)}) custom-call(f32[8,128]{1,0:T(8,128)} %get-tuple-element.18.row_ref), custom_call_target="tpu_custom_call" | custom-call | tf_op jit(solution)/shard_map/pallas_call | solution.py:270
  53.0 0.5 broadcast.7
  53.5 1.4 %fusion = (f32[2,128]{1,0:T(2,128)S(1)}, f32[2,1,128]{2,1,0:T(1,128)S(1)}) fusion(f32[]{:T(128)} %broadcast.7, f32[2,8,128]{2,1,0:T(8,128)} %get-tuple-element.20), kind=kLoop, calls=%fused_computation.6 | loop fusion | flops 256 | bytes 4100 | tf_op jit(solution)/shard_map/div | solution.py:350
  54.9 0.7 %reshape.37 = f32[4,4,8]{2,1,0:T(4,128)} reshape(f32[128]{0:T(128)S(1)} %dynamic-slice_reduce_fusion) | data formatting | bytes 1024 | tf_op jit(solution)/shard_map/reshape | solution.py:356
  55.6 0.1 div.15
  55.8 0.6 broadcast_multiply_fusion
  56.3 0.0 collective-permute-done.2.low_ref
  56.4 0.0 collective-permute-done.3.high_ref
  56.4 0.0 copy-start.1
  56.4 0.8 %copy-done = f32[8,128,128]{2,1,0:T(8,128)} copy-done((f32[8,128,128]{2,1,0:T(8,128)}, f32[8,128,128]{2,1,0:T(8,128)S(1)}, u32[]{:S(2)}) %copy-start) | copy-done | bytes 524312
  57.1 0.2 copy-done.1
  57.3 4.2 %shard_map.107 = f32[16,8,4096]{2,1,0:T(8,128)} custom-call(f32[32,128,128]{2,1,0:T(8,128)} %get-tuple-element.15.raw_ref, f32[8,128,128]{2,1,0:T(8,128)} %copy-done, f32[8,128,128]{2,1,0:T(8,128)} %copy-done.1, f32[1,4096]{1,0:T(1,128)} %bitcast.11, f32[128,128]{1,0:T(8,128)} %get-tuple-element.19.fix_ref), custom_call_target="tpu_custom_call" | custom-call | tf_op jit(solution)/shard_map/pallas_call | solution.py:303
  (4 shorter events, 0.0 us)
Async XLA Ops:
  1.4 21.9 %copy-start.2 = (s32[32,24]{1,0:T(8,128)}, s32[32,24]{1,0:T(8,128)S(1)}, u32[]{:S(2)}) copy-start(s32[32,24]{1,0:T(8,128)S(1)} %copy.14.tile_of) | copy-start | bytes 9220
  2.2 21.1 %copy-start.3 = (s32[32,24]{1,0:T(8,128)}, s32[32,24]{1,0:T(8,128)S(1)}, u32[]{:S(2)}) copy-start(s32[32,24]{1,0:T(8,128)S(1)} %copy.15.block_of) | copy-start | bytes 9220
  3.0 13.8 %collective-permute-start = (s32[8,49]{1,0:T(8,128)S(1)}, s32[8,49]{1,0:T(8,128)S(1)}, u32[]{:S(2)}, u32[]{:S(2)}) collective-permute-start(s32[8,49]{1,0:T(8,128)S(1)} %get-tuple-element.24), channel_id=1, source_target_pairs={{4,0},{8,4},{12,8},{5,1},{9,5},{13,9},{6,2},{10,6},{14,10},{7,3},{... | collective-permute-start | bytes 4712 | tf_op jit(solution)/shard_map/ppermute | solution.py:331
  4.3 12.5 %collective-permute-start.1 = (s32[8,49]{1,0:T(8,128)S(1)}, s32[8,49]{1,0:T(8,128)S(1)}, u32[]{:S(2)}, u32[]{:S(2)}) collective-permute-start(s32[8,49]{1,0:T(8,128)S(1)} %get-tuple-element.23), channel_id=1, source_target_pairs={{0,4},{4,8},{8,12},{1,5},{5,9},{9,13},{2,6},{6,10},{10,14},{3,7},{... | collective-permute-start | bytes 4712 | tf_op jit(solution)/shard_map/ppermute | solution.py:332
  16.8 0.6 copy-start.4
  16.9 0.6 copy-start.5
  23.4 33.0 %collective-permute-start.2 = (f32[8,128,128]{2,1,0:T(8,128)}, f32[8,128,128]{2,1,0:T(8,128)S(1)}, u32[]{:S(2)}, u32[]{:S(2)}) collective-permute-start(f32[8,128,128]{2,1,0:T(8,128)} %get-tuple-element.16), channel_id=1, source_target_pairs={{0,4},{4,8},{8,12},{1,5},{5,9},{9,13},{2,6},{6,10},{10,14},{3,7},{... | collective-permute-start | bytes 1572872 | tf_op jit(solution)/shard_map/ppermute | solution.py:343
  27.9 28.5 %collective-permute-start.3 = (f32[8,128,128]{2,1,0:T(8,128)}, f32[8,128,128]{2,1,0:T(8,128)S(1)}, u32[]{:S(2)}, u32[]{:S(2)}) collective-permute-start(f32[8,128,128]{2,1,0:T(8,128)} %get-tuple-element.17), channel_id=1, source_target_pairs={{4,0},{8,4},{12,8},{5,1},{9,5},{13,9},{6,2},{10,6},{14,10},{7,3},{... | collective-permute-start | bytes 1572872 | tf_op jit(solution)/shard_map/ppermute | solution.py:344
  56.4 0.8 %copy-start = (f32[8,128,128]{2,1,0:T(8,128)}, f32[8,128,128]{2,1,0:T(8,128)S(1)}, u32[]{:S(2)}) copy-start(f32[8,128,128]{2,1,0:T(8,128)S(1)} %collective-permute-done.2.low_ref) | copy-start | bytes 1572868
  56.4 1.0 %copy-start.1 = (f32[8,128,128]{2,1,0:T(8,128)}, f32[8,128,128]{2,1,0:T(8,128)S(1)}, u32[]{:S(2)}) copy-start(f32[8,128,128]{2,1,0:T(8,128)S(1)} %collective-permute-done.3.high_ref) | copy-start | bytes 1572868

commit v2 on v0

v2 whole, which is shorter than its diff:
```python
import functools

import jax
import jax.numpy as jnp
from jax import lax
from jax.experimental import pallas as pl
from jax.experimental.pallas import tpu as pltpu
from jax.sharding import PartitionSpec as P

HALO_BLK = 32
OWN_UNROLL = 2
SEND_TYPE = jnp.float32
MESH = pl.DeviceIdType.MESH
HBM = pl.BlockSpec(memory_space=pltpu.HBM)
VMEM = pl.BlockSpec(memory_space=pltpu.VMEM)


def row_of(sums):
    return jnp.sum(sums.T, axis=0, keepdims=True)


def slot_dot(source, held, table, n, slots, shift, low, high):
    tiles, blocks, live = table
    used, zero_tile = live(n), held.shape[0] - 1
    left, right = [], []
    for k in range(slots):
        block = blocks(k, n) - shift
        keep = (k < used) & (block >= low) & (block < high)
        left.append(source[jnp.where(keep, block, low)])
        right.append(held[jnp.where(keep, tiles(k, n), zero_tile)])
    return jnp.dot(
        jnp.concatenate(left, axis=1),
        jnp.concatenate(right, axis=0),
        preferred_element_type=jnp.float32,
    )


def main_kernel(
    bands, mems, edge,
    fields, mask_h, area_h, target_area_h, tiles, tile_h, block_h, live_h,
    raw, totals, fix_ref,
    mask, area, target_area, tile_s, block_s, live_s,
    stage, source, held, made, came, rows, landed, target_sum,
    tile_in, block_in, live_in, tile_n, block_n, live_n,
    load_sem, small_sem, list_sem, table_send, table_recv, edge_send, edge_recv, row_send, row_recv,
):
    band, mem = lax.axis_index("band"), lax.axis_index("mem")
    count = bands * mems
    me = mem * bands + band
    own, columns, tile = source.shape
    slots, targets = tile_h.shape
    has_low, has_high = band > 0, band < bands - 1
    chunk = HALO_BLK * tile
    chunks = own // HALO_BLK
    order = [0, chunks - 1] + list(range(1, chunks - 1))

    loads = [
        pltpu.make_async_copy(
            fields.at[:, :, pl.ds(c * chunk, chunk)],
            stage.at[:, :, pl.ds(c * chunk, chunk)],
            load_sem.at[c],
        )
        for c in range(chunks)
    ]
    small = [
        pltpu.make_async_copy(a, b, small_sem.at[i])
        for i, (a, b) in enumerate((
            (mask_h, mask),
            (area_h, area),
            (tiles, held.at[pl.ds(0, tiles.shape[0])]),
            (tile_h, tile_s),
            (block_h, block_s),
            (live_h, live_s),
            (target_area_h, target_area),
        ))
    ]
    small[0].start()
    small[1].start()
    for c in order[:2]:
        loads[c].start()
    for copy in small[2:]:
        copy.start()
    for c in order[2:]:
        loads[c].start()

    def place(step):
        other = lax.rem(me + step, count)
        return {"mem": other // bands, "band": lax.rem(other, bands)}

    barrier = pltpu.get_barrier_semaphore()

    def greet(step, carry):
        pl.semaphore_signal(barrier, inc=1, device_id=place(step), device_id_type=MESH)
        return carry

    lax.fori_loop(1, count, greet, 0)
    pl.semaphore_wait(barrier, count - 1)

    def table_copies(way):
        to = {"band": band - 1 if way == 0 else band + 1}
        pairs = ((tile_h, tile_in), (block_h, block_in), (live_h, live_in))
        return [
            pltpu.make_async_remote_copy(
                src_ref=mine,
                dst_ref=theirs.at[way],
                send_sem=table_send.at[way, i],
                recv_sem=table_recv.at[way, i],
                device_id=to,
                device_id_type=MESH,
            )
            for i, (mine, theirs) in enumerate(pairs)
        ]

    def edge_copy(way, j):
        return pltpu.make_async_remote_copy(
            src_ref=made.at[way, j],
            dst_ref=came.at[way, j],
            send_sem=edge_send.at[way, j],
            recv_sem=edge_recv.at[way, j],
            device_id={"band": band + 1 if way == 0 else band - 1},
            device_id_type=MESH,
        )

    for way, there in ((0, has_low), (1, has_high)):
        @pl.when(there)
        def _(way=way):
            for copy in table_copies(way):
                copy.start()

    held[tiles.shape[0]] = jnp.zeros((tile, tile), held.dtype)
    target_sum[...] = jnp.zeros_like(target_sum)

    def weigh(c, running):
        loads[c].wait()

        def one(n, running):
            at = pl.ds(pl.multiple_of(n * tile, tile), tile)
            scale = area[:, at] * mask[:, at].astype(jnp.float32)
            part = stage[:, :, at].astype(jnp.float32).reshape(columns, tile) * scale
            part = part.astype(source.dtype)
            source[n] = part
            return running + part.astype(jnp.float32)

        return lax.fori_loop(c * HALO_BLK, (c + 1) * HALO_BLK, one, running, unroll=4)

    source_sum = jnp.zeros((columns, tile), jnp.float32)
    small[0].wait()
    small[1].wait()
    for c in order[:2]:
        source_sum = weigh(c, source_sum)
    for copy in small[2:]:
        copy.wait()

    for way, there in ((0, has_high), (1, has_low)):
        @pl.when(there)
        def _(way=way):
            for copy in table_copies(way):
                copy.wait_recv()
            pairs = ((tile_in, tile_n), (block_in, block_n), (live_in, live_n))
            lists = [
                pltpu.make_async_copy(a.at[way], b.at[way], list_sem.at[way, i])
                for i, (a, b) in enumerate(pairs)
            ]
            for copy in lists:
                copy.start()
            for copy in lists:
                copy.wait()
            table = (
                lambda k, n: tile_n[way, k, n],
                lambda k, n: block_n[way, k, n],
                lambda n: live_n[way, 0, n],
            )
            first = 0 if way == 0 else targets - edge
            if way == 0:
                reach = (HALO_BLK - own, own - HALO_BLK, own)
            else:
                reach = (HALO_BLK + own, 0, HALO_BLK)

            def one(j, carry):
                value = slot_dot(source, held, table, first + j, slots, *reach)
                made[way, j] = value.astype(made.dtype)
                target_sum[...] += value

                @pl.when(j > 0)
                def _():
                    edge_copy(way, j - 1).start()

                return carry

            lax.fori_loop(0, edge, one, 0)

    for i, c in enumerate(order[2:]):
        source_sum = weigh(c, source_sum)
        if i == 0:
            for way, there in ((0, has_high), (1, has_low)):
                @pl.when(there)
                def _(way=way):
                    edge_copy(way, edge - 1).start()

    own_table = (
        lambda k, n: tile_s[k, n],
        lambda k, n: block_s[k, n],
        lambda n: live_s[0, n],
    )

    def own_group(g, carry):
        for u in range(OWN_UNROLL):
            t = g * OWN_UNROLL + u
            value = slot_dot(source, held, own_table, t, slots, HALO_BLK, 0, own)
            raw[t] = value
            carry = carry + value
        return carry

    target_total = lax.fori_loop(0, targets // OWN_UNROLL, own_group, target_sum[...])
    rows[0:1, :] = row_of(source_sum)
    rows[1:2, :] = row_of(target_total)
    rows[2:3, :] = jnp.broadcast_to(
        jnp.sum(target_area[...], axis=1, keepdims=True), (1, columns)
    )
    rows[3:8, :] = jnp.zeros((5, columns), jnp.float32)

    def divide(t, carry):
        at = pl.ds(pl.multiple_of(t * tile, tile), tile)
        raw[t] = raw[t] / target_area[:, at]
        return carry

    lax.fori_loop(edge, targets - edge, divide, 0, unroll=4)

    def row_copy(step):
        return pltpu.make_async_remote_copy(
            src_ref=rows,
            dst_ref=landed.at[step],
            send_sem=row_send.at[step],
            recv_sem=row_recv.at[step],
            device_id=place(step),
            device_id_type=MESH,
        )

    def begin(step, carry):
        row_copy(step).start()
        return carry

    def end(step, carry):
        row_copy(step).wait()
        return carry

    lax.fori_loop(1, count, begin, 0)
    landed[0] = rows[...]

    for way, there in ((0, has_low), (1, has_high)):
        @pl.when(there)
        def _(way=way):
            def add(j, carry):
                edge_copy(way, j).wait_recv()
                t = j if way == 0 else targets - edge + j
                raw[t] = raw[t] + came[way, j].astype(jnp.float32)
                return carry

            lax.fori_loop(0, edge, add, 0)

    lax.fori_loop(0, edge, divide, 0, unroll=4)
    lax.fori_loop(targets - edge, targets, divide, 0, unroll=4)

    for way, there in ((0, has_low), (1, has_high)):
        @pl.when(there)
        def _(way=way):
            for copy in table_copies(way):
                copy.wait_send()

    for way, there in ((0, has_high), (1, has_low)):
        @pl.when(there)
        def _(way=way):
            def sent(j, carry):
                edge_copy(way, j).wait_send()
                return carry

            lax.fori_loop(0, edge, sent, 0)

    lax.fori_loop(1, count, end, 0)
    for m in range(mems):
        total = jnp.zeros(rows.shape, jnp.float32)
        for b in range(bands):
            total = total + landed[lax.rem(me - (m * bands + b) + count, count)]
        totals[m] = total
    mine = totals[mem]
    fix = (mine[0:1, :] - mine[1:2, :]) / mine[2:3, :]
    fix_ref[...] = jnp.broadcast_to(fix, (fix_ref.shape[1], fix.shape[1])).T


def main_call(fields, mask, area, target_area, tiles, tile_t, block_t, live):
    bands, mems = lax.axis_size("band"), lax.axis_size("mem")
    rows, snaps, cells = fields.shape
    columns = rows * snaps
    slots, targets = tile_t.shape
    count, tile = tiles.shape[0], tiles.shape[1]
    own = cells // tile
    edge = HALO_BLK // (own // targets)
    dma = pltpu.SemaphoreType.DMA
    peers = bands * mems
    return pl.pallas_call(
        functools.partial(main_kernel, bands, mems, edge),
        in_specs=[HBM] * 8,
        out_specs=(VMEM, VMEM, VMEM),
        out_shape=(
            jax.ShapeDtypeStruct((targets, columns, tile), jnp.float32),
            jax.ShapeDtypeStruct((mems, 8, columns), jnp.float32),
            jax.ShapeDtypeStruct((columns, tile), jnp.float32),
        ),
        scratch_shapes=[
            pltpu.VMEM(mask.shape, mask.dtype),
            pltpu.VMEM(area.shape, area.dtype),
            pltpu.VMEM(target_area.shape, target_area.dtype),
            pltpu.SMEM(tile_t.shape, tile_t.dtype),
            pltpu.SMEM(block_t.shape, block_t.dtype),
            pltpu.SMEM(live.shape, live.dtype),
            pltpu.VMEM(fields.shape, fields.dtype),
            pltpu.VMEM((own, columns, tile), jnp.bfloat16),
            pltpu.VMEM((count + 1, tile, tile), tiles.dtype),
            pltpu.VMEM((2, edge, columns, tile), SEND_TYPE),
            pltpu.VMEM((2, edge, columns, tile), SEND_TYPE),
            pltpu.VMEM((8, columns), jnp.float32),
            pltpu.VMEM((peers, 8, columns), jnp.float32),
            pltpu.VMEM((columns, tile), jnp.float32),
            pltpu.VMEM((2, slots, targets), jnp.int32),
            pltpu.VMEM((2, slots, targets), jnp.int32),
            pltpu.VMEM((2, 1, targets), jnp.int32),
            pltpu.SMEM((2, slots, targets), jnp.int32),
            pltpu.SMEM((2, slots, targets), jnp.int32),
            pltpu.SMEM((2, 1, targets), jnp.int32),
            dma((own // HALO_BLK,)),
            dma((7,)),
            dma((2, 3)),
            dma((2, 3)),
            dma((2, 3)),
            dma((2, edge)),
            dma((2, edge)),
            dma((peers,)),
            dma((peers,)),
        ],
        compiler_params=pltpu.CompilerParams(
            collective_id=0, has_side_effects=True, vmem_limit_bytes=32 << 20
        ),
    )(fields, mask, area, target_area, tiles, tile_t, block_t, live)


def finish_kernel(fields, snaps, raw_ref, fix_ref, totals_ref, out_ref, mean_ref, ensemble_ref):
    count, columns, tile = raw_ref.shape
    fix = fix_ref[...]
    for n in range(count):
        value = raw_ref[n] + fix
        out_ref[:, :, n * tile:(n + 1) * tile] = value.reshape(columns // snaps, snaps, tile)

    @pl.when(pl.program_id(0) == 0)
    def _():
        mems, members = totals_ref.shape[0], mean_ref.shape[0]
        spot = lax.broadcasted_iota(jnp.int32, (columns, tile), 0)
        lane = lax.broadcasted_iota(jnp.int32, (columns, tile), 1)
        chosen = lax.rem(spot, snaps) == lane
        summed = jnp.zeros((fields, snaps), jnp.float32)

        def table(m):
            row = totals_ref[m, 0:1, :] / totals_ref[m, 2:3, :]
            column = jnp.broadcast_to(row, (tile, columns)).T
            spread = jnp.where(chosen, column, 0.0).reshape(columns // snaps, snaps, tile)
            return jnp.sum(spread, axis=1)[:, 0:snaps]

        mine = table(lax.axis_index("mem"))
        for n in range(members):
            mean_ref[n] = mine[n * fields:(n + 1) * fields]
        for m in range(mems):
            all_of = table(m)
            for n in range(members):
                summed = summed + all_of[n * fields:(n + 1) * fields]
        ensemble_ref[...] = summed / (mems * members)


def finish(raw, fix, totals, members, fields, snaps):
    targets, columns, tile = raw.shape
    steps = 4
    part = targets // steps
    rows = members * fields
    return pl.pallas_call(
        functools.partial(finish_kernel, fields, snaps),
        grid=(steps,),
        in_specs=[
            pl.BlockSpec((part, columns, tile), lambda i: (i, 0, 0)),
            pl.BlockSpec((columns, tile), lambda i: (0, 0)),
            pl.BlockSpec(totals.shape, lambda i: (0, 0, 0)),
        ],
        out_specs=(
            pl.BlockSpec((rows, snaps, part * tile), lambda i: (0, 0, i)),
            pl.BlockSpec((members, fields, snaps), lambda i: (0, 0, 0)),
            pl.BlockSpec((fields, snaps), lambda i: (0, 0)),
        ),
        out_shape=(
            jax.ShapeDtypeStruct((rows, snaps, targets * tile), jnp.float32),
            jax.ShapeDtypeStruct((members, fields, snaps), jnp.float32),
            jax.ShapeDtypeStruct((fields, snaps), jnp.float32),
        ),
        compiler_params=pltpu.CompilerParams(vmem_limit_bytes=16 << 20),
    )(raw, fix, totals)


def on_device(
    surface_fields, land_mask, source_area, target_area, weight_tiles, tile_of, block_of, live_slots
):
    members, fields, snaps, cells = surface_fields.shape
    targets = tile_of.shape[0]
    target_cells = target_area.shape[0]
    raw, totals, fix = main_call(
        surface_fields.reshape(members * fields, snaps, cells),
        land_mask.reshape(1, cells),
        source_area.reshape(1, cells),
        target_area.reshape(1, target_cells),
        weight_tiles,
        tile_of.T,
        block_of.T,
        live_slots.reshape(1, targets),
    )
    regridded, conserved, ensemble = finish(raw, fix, totals, members, fields, snaps)
    return regridded.reshape(members, fields, snaps, target_cells), conserved, ensemble


def solution(mesh):
    placed = (
        P(("grp", "mem"), "fld", None, "band"),
        P("band"),
        P("band"),
        P("band"),
        P(),
        P("band", None),
        P("band", None),
        P("band"),
    )
    return jax.shard_map(
        on_device,
        mesh=mesh,
        in_specs=placed,
        out_specs=(
            P(("grp", "mem"), "fld", None, "band"),
            P(("grp", "mem"), "fld", None),
            P(("grp", "fld"), None),
        ),
        check_vma=False,
    )
```

time: 306 us -> 41.3 us (0.13)
  local copies, waits for them, and re-layouts: 128 us -> 7.68 us
  matrix products: 91.6 us -> 0 us
  other arithmetic: 35.9 us -> 0 us
  Pallas kernels: 0 us -> 32.5 us
  waiting for transfers between devices: 24.5 us -> 0 us
  blocking collectives: 15.5 us -> 0 us
  starting transfers between devices: 6.3 us -> 0 us
    gather x48 -> x0, local copies, waits for them, and re-layouts: 103 us -> none  [the longest x24 84.8 us: one_slot(): chosen = jnp.take(source, picked[:, position], axis=1)]
    dot_general x24 -> x0, matrix products: 91.6 us -> none  [one_slot(): jnp.einsum('cnb,nbd->cnd', chosen, weights, preferred_element_type=jnp.fl...]
    pallas_call x0 -> x2, Pallas kernels: none -> 32.5 us  [the longest x1 30.4 us: main_call(): pl.pallas_call(functools.partial(main_kernel, bands, mems, edge), in_spec...]
    ppermute x2 -> x0, waiting for transfers between devices: 24.5 us -> none  [the longest x1 20.6 us: extended_2(): before = lax.ppermute(last, axis, up)]
    reduce_and x24 -> x0, other arithmetic: 17.1 us -> none  [one_slot(): chosen = jnp.take(source, picked[:, position], axis=1)]
    psum x2 -> x0, blocking collectives: 15.5 us -> none  [the longest x1 10.5 us: band_totals(): return lax.psum((own_total, target_part, area_part), 'band')]
    concatenate x1 -> x0, local copies, waits for them, and re-layouts: 8.62 us -> none  [extended_2(): array = jnp.concatenate([before, array, after], axis=dim)]
    concatenate x1 -> x0, other arithmetic: 6.76 us -> none  [extended_2(): array = jnp.concatenate([before, array, after], axis=dim)]
  transfers between devices with their start and end apart: 2 -> 0, of which waited for: 2 -> 0; matrix products, arithmetic and copies ran while one was open for 0% -> 0% of each run, Pallas kernels for 0% -> 0%
where the time goes in v2:
time: 41.3 us; the launch traced here: 40.8 us
  Pallas kernels  32.5 us (79%)
  local copies, waits for them, and re-layouts  7.68 us (19%)
  between operations  0.66 us (2%)
    pallas_call x1, Pallas kernels, main_call(): pl.pallas_call(functools.partial(main_kernel, bands, mems, edge), in_spec...  30.4 us
    unnamed x16, local copies, waits for them, and re-layouts  7.68 us
    pallas_call x1, Pallas kernels, finish(): pl.pallas_call(functools.partial(finish_kernel, fields, snaps), grid=(ste...  2.05 us

profile of v2, /device:TPU:0, one launch (start us, length us, event | category | flops | bytes accessed | tf_op | source)
XLA Modules:
  0.0 40.8 jit_solution(8133875731497427659)
XLA Ops:
  0.6 0.0 copy-start
  0.6 2.2 %copy-done = bf16[4,4,8,16384]{3,2,1,0:T(8,128)(2,1)S(1)} copy-done((bf16[4,4,8,16384]{3,2,1,0:T(8,128)(2,1)S(1)}, bf16[4,4,8,16384]{3,2,1,0:T(8,128)(2,1)}, u32[]{:S(2)}) %copy-start) | copy-done | bytes 4194328
  2.8 0.0 copy-start.1
  2.8 1.0 %copy-done.1 = bf16[16,128,128]{2,1,0:T(8,128)(2,1)S(1)} copy-done((bf16[16,128,128]{2,1,0:T(8,128)(2,1)S(1)}, bf16[16,128,128]{2,1,0:T(8,128)(2,1)}, u32[]{:S(2)}) %copy-start.1) | copy-done | bytes 524312
  3.9 0.0 copy-start.2
  3.9 0.8 %copy-done.2 = s32[16384]{0:T(1024)S(1)} copy-done((s32[16384]{0:T(1024)S(1)}, s32[16384]{0:T(1024)}, u32[]{:S(2)}) %copy-start.2) | copy-done | bytes 65560
  4.7 0.0 copy-start.3
  4.7 0.8 %copy-done.3 = f32[16384]{0:T(1024)S(1)} copy-done((f32[16384]{0:T(1024)S(1)}, f32[16384]{0:T(1024)}, u32[]{:S(2)}) %copy-start.3) | copy-done | bytes 65560
  5.5 0.0 copy-start.4
  5.5 0.7 %copy-done.4 = f32[4096]{0:T(1024)S(1)} copy-done((f32[4096]{0:T(1024)S(1)}, f32[4096]{0:T(1024)}, u32[]{:S(2)}) %copy-start.4) | copy-done | bytes 16408
  6.3 0.0 copy-start.5
  6.3 0.7 %copy-done.5 = s32[32,24]{0,1:T(8,128)S(1)} copy-done((s32[32,24]{0,1:T(8,128)S(1)}, s32[32,24]{0,1:T(8,128)}, u32[]{:S(2)}) %copy-start.5) | copy-done | bytes 3096
  7.0 0.0 copy-start.6
  7.0 0.7 %copy-done.6 = s32[32,24]{0,1:T(8,128)S(1)} copy-done((s32[32,24]{0,1:T(8,128)S(1)}, s32[32,24]{0,1:T(8,128)}, u32[]{:S(2)}) %copy-start.6) | copy-done | bytes 3096
  7.7 0.0 copy-start.7
  7.7 0.7 %copy-done.7 = s32[32]{0:T(128)S(1)} copy-done((s32[32]{0:T(128)S(1)}, s32[32]{0:T(128)}, u32[]{:S(2)}) %copy-start.7) | copy-done | bytes 152
  8.3 30.4 %shard_map.103 = (f32[32,128,128]{2,1,0:T(8,128)S(1)}, f32[2,8,128]{2,1,0:T(8,128)S(1)}, f32[128,128]{1,0:T(8,128)S(1)}) custom-call(bf16[16,8,16384]{2,1,0:T(8,128)(2,1)S(1)} %bitcast.8, s32[1,16384]{1,0:T(1,128)S(1)} %bitcast.9, f32[1,16384]{1,0:T(1,128)S(1)} %bitcast.10, f32[1,4096]{1,0:T(1,128)S(1)} %bitcast.11, bf16[16,128,128]{2,1,0:T(8,128)(2,1)S(1)} %copy-done.1, ...), custom_call_target="tpu_custom_call" | custom-call | tf_op jit(solution)/shard_map/pallas_call | solution.py:300
  38.8 2.1 %shard_map.104 = (f32[16,8,4096]{2,1,0:T(8,128)}, f32[4,4,8]{2,1,0:T(4,128)}, f32[4,8]{1,0:T(4,128)}) custom-call(f32[32,128,128]{2,1,0:T(8,128)S(1)} %get-tuple-element.9.raw_ref, f32[128,128]{1,0:T(8,128)S(1)} %get-tuple-element.10.fix_ref, f32[2,8,128]{2,1,0:T(8,128)S(1)} %get-tuple-element.11.totals_ref), custom_call_target="tpu_custom_call" | custom-call | tf_op jit(solution)/shard_map/pallas_call | solution.py:382
Async XLA Ops:
  0.6 2.2 %copy-start = (bf16[4,4,8,16384]{3,2,1,0:T(8,128)(2,1)S(1)}, bf16[4,4,8,16384]{3,2,1,0:T(8,128)(2,1)}, u32[]{:S(2)}) copy-start(bf16[4,4,8,16384]{3,2,1,0:T(8,128)(2,1)} %param.8) | copy-start | bytes 12582916
  2.8 1.0 %copy-start.1 = (bf16[16,128,128]{2,1,0:T(8,128)(2,1)S(1)}, bf16[16,128,128]{2,1,0:T(8,128)(2,1)}, u32[]{:S(2)}) copy-start(bf16[16,128,128]{2,1,0:T(8,128)(2,1)} %tiles.1) | copy-start | bytes 1572868
  3.9 0.8 %copy-start.2 = (s32[16384]{0:T(1024)S(1)}, s32[16384]{0:T(1024)}, u32[]{:S(2)}) copy-start(s32[16384]{0:T(1024)} %param.9) | copy-start | bytes 196612
  4.7 0.8 %copy-start.3 = (f32[16384]{0:T(1024)S(1)}, f32[16384]{0:T(1024)}, u32[]{:S(2)}) copy-start(f32[16384]{0:T(1024)} %param.10) | copy-start | bytes 196612
  5.5 0.7 %copy-start.4 = (f32[4096]{0:T(1024)S(1)}, f32[4096]{0:T(1024)}, u32[]{:S(2)}) copy-start(f32[4096]{0:T(1024)} %param.11) | copy-start | bytes 49156
  6.3 0.7 %copy-start.5 = (s32[32,24]{0,1:T(8,128)S(1)}, s32[32,24]{0,1:T(8,128)}, u32[]{:S(2)}) copy-start(s32[32,24]{0,1:T(8,128)} %param.13) | copy-start | bytes 9220
  7.0 0.7 %copy-start.6 = (s32[32,24]{0,1:T(8,128)S(1)}, s32[32,24]{0,1:T(8,128)}, u32[]{:S(2)}) copy-start(s32[32,24]{0,1:T(8,128)} %param.14) | copy-start | bytes 9220
  7.7 0.7 %copy-start.7 = (s32[32]{0:T(128)S(1)}, s32[32]{0:T(128)}, u32[]{:S(2)}) copy-start(s32[32]{0:T(128)} %param.15) | copy-start | bytes 388

commit v3 on v2

--- a/solution.py
+++ b/solution.py
@@ -340,7 +340,7 @@
         compiler_params=pltpu.CompilerParams(
             collective_id=0, has_side_effects=True, vmem_limit_bytes=32 << 20
         ),
-    )(fields, mask, area, target_area, tiles, tile_t, block_t, live)
+    )(*[pltpu.with_memory_space_constraint(a, pltpu.HBM) for a in (fields, mask, area, target_area, tiles, tile_t, block_t, live)])
 
 
 def finish_kernel(fields, snaps, raw_ref, fix_ref, totals_ref, out_ref, mean_ref, ensemble_ref):

time: 41.3 us -> 33.1 us (0.80)
  local copies, waits for them, and re-layouts: 7.68 us -> 0 us
    unnamed x16 -> x0, local copies, waits for them, and re-layouts: 7.68 us -> none
where the time goes in v3:
time: 33.1 us; the launch traced here: 32.9 us
  Pallas kernels  32.3 us (98%)
  between operations  0.64 us (2%)
    pallas_call x1, Pallas kernels, main_call(): pl.pallas_call(functools.partial(main_kernel, bands, mems, edge), in_spec...  30.2 us
    pallas_call x1, Pallas kernels, finish(): pl.pallas_call(functools.partial(finish_kernel, fields, snaps), grid=(ste...  2.05 us

profile of v3, /device:TPU:0, one launch (start us, length us, event | category | flops | bytes accessed | tf_op | source)
XLA Modules:
  0.0 32.9 jit_solution(14377900909182680561)
XLA Ops:
  0.6 30.2 %shard_map.103 = (f32[32,128,128]{2,1,0:T(8,128)S(1)}, f32[2,8,128]{2,1,0:T(8,128)S(1)}, f32[128,128]{1,0:T(8,128)S(1)}) custom-call(bf16[16,8,16384]{2,1,0:T(8,128)(2,1)} %bitcast.8, s32[1,16384]{1,0:T(1,128)} %bitcast.9, f32[1,16384]{1,0:T(1,128)} %bitcast.10, f32[1,4096]{1,0:T(1,128)} %bitcast.11, bf16[16,128,128]{2,1,0:T(8,128)(2,1)} %tiles.1, ...), custom_call_target="tpu_custom_call" | custom-call | tf_op jit(solution)/shard_map/pallas_call | solution.py:300
  30.9 2.1 %shard_map.104 = (f32[16,8,4096]{2,1,0:T(8,128)}, f32[4,4,8]{2,1,0:T(4,128)}, f32[4,8]{1,0:T(4,128)}) custom-call(f32[32,128,128]{2,1,0:T(8,128)S(1)} %get-tuple-element.9.raw_ref, f32[128,128]{1,0:T(8,128)S(1)} %get-tuple-element.10.fix_ref, f32[2,8,128]{2,1,0:T(8,128)S(1)} %get-tuple-element.11.totals_ref), custom_call_target="tpu_custom_call" | custom-call | tf_op jit(solution)/shard_map/pallas_call | solution.py:382

commit v4 on v3

--- a/solution.py
+++ b/solution.py
@@ -8,7 +8,7 @@
 from jax.sharding import PartitionSpec as P
 
 HALO_BLK = 32
-OWN_UNROLL = 2
+OWN_UNROLL = 4
 SEND_TYPE = jnp.float32
 MESH = pl.DeviceIdType.MESH
 HBM = pl.BlockSpec(memory_space=pltpu.HBM)
@@ -128,7 +128,15 @@
                 copy.start()
 
     held[tiles.shape[0]] = jnp.zeros((tile, tile), held.dtype)
-    target_sum[...] = jnp.zeros_like(target_sum)
+
+    def fetch(pairs):
+        copies = [
+            pltpu.make_async_copy(a, b, list_sem.at[i]) for i, (a, b) in enumerate(pairs)
+        ]
+        for copy in copies:
+            copy.start()
+        for copy in copies:
+            copy.wait()
 
     def weigh(c, running):
         loads[c].wait()
@@ -157,37 +165,39 @@
             for copy in table_copies(way):
                 copy.wait_recv()
             pairs = ((tile_in, tile_n), (block_in, block_n), (live_in, live_n))
-            lists = [
-                pltpu.make_async_copy(a.at[way], b.at[way], list_sem.at[way, i])
-                for i, (a, b) in enumerate(pairs)
-            ]
-            for copy in lists:
-                copy.start()
-            for copy in lists:
-                copy.wait()
+            fetch([(a.at[way], b.at[way]) for a, b in pairs])
+
+        @pl.when(jnp.logical_not(there))
+        def _(way=way):
+            pairs = ((tile_h, tile_n), (block_h, block_n), (live_h, live_n))
+            fetch([(a, b.at[way]) for a, b in pairs])
+
+    reaches = (
+        (HALO_BLK - own, own - HALO_BLK, own),
+        (HALO_BLK + own, 0, HALO_BLK),
+    )
+
+    def one_edge(j, carry):
+        for way, there in ((0, has_high), (1, has_low)):
             table = (
-                lambda k, n: tile_n[way, k, n],
-                lambda k, n: block_n[way, k, n],
-                lambda n: live_n[way, 0, n],
+                lambda k, n, way=way: tile_n[way, k, n],
+                lambda k, n, way=way: block_n[way, k, n],
+                lambda n, way=way: live_n[way, 0, n],
             )
             first = 0 if way == 0 else targets - edge
-            if way == 0:
-                reach = (HALO_BLK - own, own - HALO_BLK, own)
-            else:
-                reach = (HALO_BLK + own, 0, HALO_BLK)
-
-            def one(j, carry):
-                value = slot_dot(source, held, table, first + j, slots, *reach)
-                made[way, j] = value.astype(made.dtype)
-                target_sum[...] += value
-
-                @pl.when(j > 0)
-                def _():
-                    edge_copy(way, j - 1).start()
-
-                return carry
-
-            lax.fori_loop(0, edge, one, 0)
+            value = slot_dot(source, held, table, first + j, slots, *reaches[way])
+            made[way, j] = value.astype(made.dtype)
+            carry = carry + value * there.astype(jnp.float32)
+
+        for way, there in ((0, has_high), (1, has_low)):
+            @pl.when((j > 0) & there)
+            def _(way=way):
+                edge_copy(way, j - 1).start()
+
+        return carry
+
+    edge_total = lax.fori_loop(0, edge, one_edge, jnp.zeros((columns, tile), jnp.float32))
+    target_sum[...] = edge_total
 
     for i, c in enumerate(order[2:]):
         source_sum = weigh(c, source_sum)
@@ -329,7 +339,7 @@
             pltpu.SMEM((2, 1, targets), jnp.int32),
             dma((own // HALO_BLK,)),
             dma((7,)),
-            dma((2, 3)),
+            dma((3,)),
             dma((2, 3)),
             dma((2, 3)),
             dma((2, edge)),

time: 33.1 us -> 30.6 us (0.924)
  Pallas kernels: 32.3 us -> 29.7 us
    pallas_call x1, Pallas kernels: 30.2 us -> 27.7 us  [main_call(): pl.pallas_call(functools.partial(main_kernel, bands, mems, edge), in_spec...]
where the time goes in v4:
time: 30.6 us; the launch traced here: 30.4 us
  Pallas kernels  29.7 us (97%)
  between operations  0.64 us (2%)
    pallas_call x1, Pallas kernels, main_call(): pl.pallas_call(functools.partial(main_kernel, bands, mems, edge), in_spec...  27.7 us
    pallas_call x1, Pallas kernels, finish(): pl.pallas_call(functools.partial(finish_kernel, fields, snaps), grid=(ste...  2.05 us

profile of v4, /device:TPU:0, one launch (start us, length us, event | category | flops | bytes accessed | tf_op | source)
XLA Modules:
  0.0 30.4 jit_solution(5604508258293279649)
XLA Ops:
  0.6 27.7 %shard_map.103 = (f32[32,128,128]{2,1,0:T(8,128)S(1)}, f32[2,8,128]{2,1,0:T(8,128)S(1)}, f32[128,128]{1,0:T(8,128)S(1)}) custom-call(bf16[16,8,16384]{2,1,0:T(8,128)(2,1)} %bitcast.8, s32[1,16384]{1,0:T(1,128)} %bitcast.9, f32[1,16384]{1,0:T(1,128)} %bitcast.10, f32[1,4096]{1,0:T(1,128)} %bitcast.11, bf16[16,128,128]{2,1,0:T(8,128)(2,1)} %tiles.1, ...), custom_call_target="tpu_custom_call" | custom-call | tf_op jit(solution)/shard_map/pallas_call | solution.py:310
  28.3 2.1 %shard_map.104 = (f32[16,8,4096]{2,1,0:T(8,128)}, f32[4,4,8]{2,1,0:T(4,128)}, f32[4,8]{1,0:T(4,128)}) custom-call(f32[32,128,128]{2,1,0:T(8,128)S(1)} %get-tuple-element.9.raw_ref, f32[128,128]{1,0:T(8,128)S(1)} %get-tuple-element.10.fix_ref, f32[2,8,128]{2,1,0:T(8,128)S(1)} %get-tuple-element.11.totals_ref), custom_call_target="tpu_custom_call" | custom-call | tf_op jit(solution)/shard_map/pallas_call | solution.py:392

commit v5 on v4

--- a/solution.py
+++ b/solution.py
@@ -8,7 +8,6 @@
 from jax.sharding import PartitionSpec as P
 
 HALO_BLK = 32
-OWN_UNROLL = 4
 SEND_TYPE = jnp.float32
 MESH = pl.DeviceIdType.MESH
 HBM = pl.BlockSpec(memory_space=pltpu.HBM)
@@ -53,6 +52,18 @@
     chunk = HALO_BLK * tile
     chunks = own // HALO_BLK
     order = [0, chunks - 1] + list(range(1, chunks - 1))
+
+    def place(step):
+        other = lax.rem(me + step, count)
+        return {"mem": other // bands, "band": lax.rem(other, bands)}
+
+    barrier = pltpu.get_barrier_semaphore()
+
+    def greet(step, carry):
+        pl.semaphore_signal(barrier, inc=1, device_id=place(step), device_id_type=MESH)
+        return carry
+
+    lax.fori_loop(1, count, greet, 0)
 
     loads = [
         pltpu.make_async_copy(
@@ -83,17 +94,6 @@
     for c in order[2:]:
         loads[c].start()
 
-    def place(step):
-        other = lax.rem(me + step, count)
-        return {"mem": other // bands, "band": lax.rem(other, bands)}
-
-    barrier = pltpu.get_barrier_semaphore()
-
-    def greet(step, carry):
-        pl.semaphore_signal(barrier, inc=1, device_id=place(step), device_id_type=MESH)
-        return carry
-
-    lax.fori_loop(1, count, greet, 0)
     pl.semaphore_wait(barrier, count - 1)
 
     def table_copies(way):
@@ -154,10 +154,27 @@
     source_sum = jnp.zeros((columns, tile), jnp.float32)
     small[0].wait()
     small[1].wait()
-    for c in order[:2]:
+    for c in order:
         source_sum = weigh(c, source_sum)
+
+    own_table = (
+        lambda k, n: tile_s[k, n],
+        lambda k, n: block_s[k, n],
+        lambda n: live_s[0, n],
+    )
+
+    def own_group(first, width, carry):
+        for u in range(width):
+            t = first + u
+            at = pl.ds(pl.multiple_of(t * tile, tile), tile)
+            value = slot_dot(source, held, own_table, t, slots, HALO_BLK, 0, own)
+            raw[t] = value * (1.0 / target_area[:, at])
+            carry = carry + value
+        return carry
+
     for copy in small[2:]:
         copy.wait()
+    target_sum[...] = own_group(0, edge // 2, jnp.zeros((columns, tile), jnp.float32))
 
     for way, there in ((0, has_high), (1, has_low)):
         @pl.when(there)
@@ -196,45 +213,24 @@
 
         return carry
 
-    edge_total = lax.fori_loop(0, edge, one_edge, jnp.zeros((columns, tile), jnp.float32))
+    edge_total = lax.fori_loop(0, edge, one_edge, target_sum[...])
     target_sum[...] = edge_total
 
-    for i, c in enumerate(order[2:]):
-        source_sum = weigh(c, source_sum)
-        if i == 0:
-            for way, there in ((0, has_high), (1, has_low)):
-                @pl.when(there)
-                def _(way=way):
-                    edge_copy(way, edge - 1).start()
-
-    own_table = (
-        lambda k, n: tile_s[k, n],
-        lambda k, n: block_s[k, n],
-        lambda n: live_s[0, n],
-    )
-
-    def own_group(g, carry):
-        for u in range(OWN_UNROLL):
-            t = g * OWN_UNROLL + u
-            value = slot_dot(source, held, own_table, t, slots, HALO_BLK, 0, own)
-            raw[t] = value
-            carry = carry + value
-        return carry
-
-    target_total = lax.fori_loop(0, targets // OWN_UNROLL, own_group, target_sum[...])
+    target_sum[...] = own_group(edge // 2, edge // 2, target_sum[...])
+    for way, there in ((0, has_high), (1, has_low)):
+        @pl.when(there)
+        def _(way=way):
+            edge_copy(way, edge - 1).start()
+
+    target_total = lax.fori_loop(
+        1, targets // edge, lambda g, carry: own_group(g * edge, edge, carry), target_sum[...]
+    )
     rows[0:1, :] = row_of(source_sum)
     rows[1:2, :] = row_of(target_total)
     rows[2:3, :] = jnp.broadcast_to(
         jnp.sum(target_area[...], axis=1, keepdims=True), (1, columns)
     )
     rows[3:8, :] = jnp.zeros((5, columns), jnp.float32)
-
-    def divide(t, carry):
-        at = pl.ds(pl.multiple_of(t * tile, tile), tile)
-        raw[t] = raw[t] / target_area[:, at]
-        return carry
-
-    lax.fori_loop(edge, targets - edge, divide, 0, unroll=4)
 
     def row_copy(step):
         return pltpu.make_async_remote_copy(
@@ -254,6 +250,12 @@
         row_copy(step).wait()
         return carry
 
+    for way, there in ((0, has_low), (1, has_high)):
+        @pl.when(there)
+        def _(way=way):
+            for copy in table_copies(way):
+                copy.wait_send()
+
     lax.fori_loop(1, count, begin, 0)
     landed[0] = rows[...]
 
@@ -263,19 +265,12 @@
             def add(j, carry):
                 edge_copy(way, j).wait_recv()
                 t = j if way == 0 else targets - edge + j
-                raw[t] = raw[t] + came[way, j].astype(jnp.float32)
+                at = pl.ds(pl.multiple_of(t * tile, tile), tile)
+                share = 1.0 / target_area[:, at]
+                raw[t] = raw[t] + came[way, j].astype(jnp.float32) * share
                 return carry
 
             lax.fori_loop(0, edge, add, 0)
-
-    lax.fori_loop(0, edge, divide, 0, unroll=4)
-    lax.fori_loop(targets - edge, targets, divide, 0, unroll=4)
-
-    for way, there in ((0, has_low), (1, has_high)):
-        @pl.when(there)
-        def _(way=way):
-            for copy in table_copies(way):
-                copy.wait_send()
 
     for way, there in ((0, has_high), (1, has_low)):
         @pl.when(there)
@@ -360,7 +355,7 @@
         value = raw_ref[n] + fix
         out_ref[:, :, n * tile:(n + 1) * tile] = value.reshape(columns // snaps, snaps, tile)
 
-    @pl.when(pl.program_id(0) == 0)
+    @pl.when(pl.program_id(0) == 1)
     def _():
         mems, members = totals_ref.shape[0], mean_ref.shape[0]
         spot = lax.broadcasted_iota(jnp.int32, (columns, tile), 0)
@@ -386,7 +381,7 @@
 
 def finish(raw, fix, totals, members, fields, snaps):
     targets, columns, tile = raw.shape
-    steps = 4
+    steps = 2
     part = targets // steps
     rows = members * fields
     return pl.pallas_call(

time: 30.6 us -> 28.8 us (0.941)
  Pallas kernels: 29.7 us -> 28 us
    pallas_call x1, Pallas kernels: 27.7 us -> 26.5 us  [main_call(): pl.pallas_call(functools.partial(main_kernel, bands, mems, edge), in_spec...]
    pallas_call x1, Pallas kernels: 2.05 us -> 1.46 us  [finish(): pl.pallas_call(functools.partial(finish_kernel, fields, snaps), grid=(ste...]
where the time goes in v5:
time: 28.8 us; the launch traced here: 28.6 us
  Pallas kernels  28 us (97%)
  between operations  0.64 us (2%)
    pallas_call x1, Pallas kernels, main_call(): pl.pallas_call(functools.partial(main_kernel, bands, mems, edge), in_spec...  26.5 us
    pallas_call x1, Pallas kernels, finish(): pl.pallas_call(functools.partial(finish_kernel, fields, snaps), grid=(ste...  1.46 us

profile of v5, /device:TPU:0, one launch (start us, length us, event | category | flops | bytes accessed | tf_op | source)
XLA Modules:
  0.0 28.6 jit_solution(15077263279095160401)
XLA Ops:
  0.6 26.5 %shard_map.103 = (f32[32,128,128]{2,1,0:T(8,128)S(1)}, f32[2,8,128]{2,1,0:T(8,128)S(1)}, f32[128,128]{1,0:T(8,128)S(1)}) custom-call(bf16[16,8,16384]{2,1,0:T(8,128)(2,1)} %bitcast.8, s32[1,16384]{1,0:T(1,128)} %bitcast.9, f32[1,16384]{1,0:T(1,128)} %bitcast.10, f32[1,4096]{1,0:T(1,128)} %bitcast.11, bf16[16,128,128]{2,1,0:T(8,128)(2,1)} %tiles.1, ...), custom_call_target="tpu_custom_call" | custom-call | tf_op jit(solution)/shard_map/pallas_call | solution.py:305
  27.1 1.5 %shard_map.104 = (f32[16,8,4096]{2,1,0:T(8,128)}, f32[4,4,8]{2,1,0:T(4,128)}, f32[4,8]{1,0:T(4,128)}) custom-call(f32[32,128,128]{2,1,0:T(8,128)S(1)} %get-tuple-element.9.raw_ref, f32[128,128]{1,0:T(8,128)S(1)} %get-tuple-element.10.fix_ref, f32[2,8,128]{2,1,0:T(8,128)S(1)} %get-tuple-element.11.totals_ref), custom_call_target="tpu_custom_call" | custom-call | tf_op jit(solution)/shard_map/pallas_call | solution.py:387
